TPU v7x, 256 devices: a whole 4x4x8 slice. The times are simulated.
256 devices in a mesh: row: 16 (over x_lo, y, core), col: 16 (over z, x_hi).
Axes of the slice: x: 4 (x_hi: 2, x_lo: 2; x = x_hi * 2 + x_lo), y: 4, z: 8, core: 2. Of those that a mesh axis runs over, the one named last changes fastest.
Arguments:
- matrix: float32 [12288, 12288], P('row', 'col'), as said below
- left_panel: float32 [12288, 1024], P('row', 'col'), may hold values from -2.5 to 2.5
- right_panel: float32 [12288, 1024], P('row', 'col'), may hold values from -2.5 to 2.5
- reflectors: float32 [12288, 256], P('row', 'col'), may hold values from -0.109375 to 0.109375
Outputs:
- updated: float32 [12288, 12288], P('row', 'col')
Inputs may be any that keep to these rules, and one draw needn't show every extreme that they name: matrix is exactly skew-symmetric.
All inputs are finite; a program needn't handle non-finite values.
Results may differ from a plain program's by a relative error of at most 0.00011.
Values sent between devices are 32-bit elements; how exact they have to be, the bound alone decides.
A program may use at most 128 MiB of HBM per device.

v0:
```python
import jax
import jax.numpy as jnp
from jax import lax
from jax.sharding import PartitionSpec as P


def product(first, second):
    return jnp.dot(
        first, second, precision=lax.Precision.HIGHEST, preferred_element_type=jnp.float32
    )


def outer_rows(first, second):
    return lax.dot_general(
        first,
        second,
        (((1,), (1,)), ((), ())),
        precision=lax.Precision.HIGHEST,
        preferred_element_type=jnp.float32,
    )


def split_parts(joined, k_share, nb_share, groups):
    rows = joined.shape[0]
    shaped = joined.reshape(rows, groups, 2 * k_share + nb_share)
    left_part = shaped[:, :, :k_share].reshape(rows, groups * k_share)
    right_part = shaped[:, :, k_share : 2 * k_share].reshape(rows, groups * k_share)
    refl_part = shaped[:, :, 2 * k_share :].reshape(rows, groups * nb_share)
    return (left_part, right_part, refl_part)


def column_rows(share):
    gathered = lax.all_gather(share, "row", axis=0, tiled=True)
    return lax.all_to_all(gathered, "col", split_axis=0, concat_axis=1, tiled=True)


def local(matrix, left_panel, right_panel, reflectors):
    col_index = lax.axis_index("col")
    groups = lax.axis_size("col")
    k_share = left_panel.shape[1]
    nb_share = reflectors.shape[1]
    joined = jnp.concatenate([left_panel, right_panel, reflectors], axis=1)
    row_joined = lax.all_gather(joined, "col", axis=1, tiled=True)
    row_left, row_right, row_refl = split_parts(row_joined, k_share, nb_share, groups)
    col_joined = column_rows(joined)
    col_left, col_right, col_refl = split_parts(col_joined, k_share, nb_share, groups)
    reduced = matrix - outer_rows(row_left, col_right) + outer_rows(row_right, col_left)
    image_rows = lax.psum(product(reduced, col_refl), "col")
    image_share = lax.dynamic_slice_in_dim(image_rows, col_index * nb_share, nb_share, 1)
    image_cols = column_rows(image_share)
    return reduced + outer_rows(row_refl, image_cols) - outer_rows(image_rows, col_refl)


def solution(mesh):
    in_specs = (P("row", "col"), P("row", "col"), P("row", "col"), P("row", "col"))
    out_specs = P("row", "col")
    return jax.shard_map(local, mesh=mesh, in_specs=in_specs, out_specs=out_specs, check_vma=False)
```

profile of v0, /device:TPU:8, one launch (start us, length us, event | category | flops | bytes accessed | tf_op | source)
XLA Modules:
  0.0 579.2 jit_solution(7612680755275399998)
XLA Ops:
  7.4 0.0 all-gather.5.cloned.1.call-start
  7.4 0.9 constant_dynamic-update-slice_fusion.2
  8.3 0.9 constant_dynamic-update-slice_fusion.1
  9.3 0.8 constant_dynamic-update-slice_fusion
  10.1 0.0 copy-start
  10.1 0.8 copy-done
  10.8 0.0 all-gather.5.cloned.1.call-update
  10.9 51.5 %all-gather.5.cloned.1.call-done = f32[12288,144]{0,1:T(8,128)} async-done(((f32[768,144]{0,1:T(8,128)}), f32[12288,144]{0,1:T(8,128)}) %all-gather.5.cloned.1.call-update) | async-done | bytes 7077904 | tf_op jit(solution)/shard_map/all_gather | solution.py:33
  62.3 6.7 %copy.10 = f32[18,16,8,768]{3,2,0,1:T(8,128)} copy(f32[18,16,8,768]{3,2,1,0:T(8,128)} %bitcast.27) | data formatting | bytes 14155776 | tf_op jit(solution)/shard_map/all_to_all | solution.py:34
  69.0 9.6 %all-to-all-start = ((f32[16,768,144]{1,2,0:T(8,128)}), f32[16,768,144]{1,2,0:T(8,128)}, u32[]{:S(2)}, u32[]{:S(2)}) async-start(f32[16,768,144]{1,2,0:T(8,128)} %bitcast.25), calls=%async_computation | async-start | bytes 14155776 | tf_op jit(solution)/shard_map/all_to_all | solution.py:34
  78.6 0.0 all-gather.3.cloned.1.call-start
  78.6 0.5 all-gather.3.cloned.1.call-update
  79.1 0.0 all-reduce.2.cloned.1.call-start
  79.2 188.7 %all-to-all-done = f32[16,768,144]{1,2,0:T(8,128)} async-done(((f32[16,768,144]{1,2,0:T(8,128)}), f32[16,768,144]{1,2,0:T(8,128)}, u32[]{:S(2)}, u32[]{:S(2)}) %all-to-all-start) | async-done | bytes 7077920 | tf_op jit(solution)/shard_map/all_to_all | solution.py:34
  267.9 1.2 slice.29
  269.1 33.7 %all-gather.3.cloned.1.call-done = f32[768,2304]{0,1:T(8,128)} async-done(((f32[768,144]{0,1:T(8,128)}), f32[768,2304]{0,1:T(8,128)}) %all-gather.3.cloned.1.call-update) | async-done | bytes 7077904 | tf_op jit(solution)/shard_map/all_gather | solution.py:43
  302.8 0.0 copy-start.1
  302.8 10.8 %fusion = f32[768,768,1]{1,0,2:T(8,128)S(1)} fusion(f32[768,16,144]{0,2,1:T(8,128)} %bitcast.1, f32[768,16,144]{0,2,1:T(8,128)} %bitcast.30), kind=kOutput, calls=%fused_computation.1 | convolution fusion | flops 7247757312 | bytes 8650752 | tf_op jit(solution)/shard_map/dot_general | solution.py:14
  313.7 0.0 copy-done.1
  313.7 11.1 %bitcast_add_fusion.1 = f32[768,768]{1,0:T(8,128)S(1)} fusion(f32[768,768,1]{1,0,2:T(8,128)S(1)} %fusion, f32[768,768]{1,0:T(8,128)S(1)} %copy-done.1, f32[768,16,144]{0,2,1:T(8,128)} %bitcast.1, f32[768,16,144]{0,2,1:T(8,128)} %bitcast.31), kind=kOutput, calls=%fused_computation.9 | convolution fusion | flops 7248936960 | bytes 13369344 | tf_op jit(solution)/shard_map/dot_general | solution.py:14
  324.8 2.9 fusion.13
  327.7 0.0 all-reduce.2.cloned.1.call-update
  327.7 155.7 %all-reduce.2.cloned.1.call-done = f32[768,256]{1,0:T(8,128)} async-done(((f32[768,256]{1,0:T(8,128)}), f32[768,256]{1,0:T(8,128)}) %all-reduce.2.cloned.1.call-update) | async-done | bytes 786448 | tf_op jit(solution)/shard_map/psum | solution.py:48
  483.5 1.2 constant_dynamic-slice_fusion
  484.6 43.6 %all_gather.11 = f32[12288,16]{1,0:T(8,128)} all-gather(f32[768,16]{1,0:T(8,128)S(1)} %constant_dynamic-slice_fusion), channel_id=1, replica_groups=mesh['row'=16,'col'=16] {'row'}, dimensions={0}, use_global_device_ids=true | all-gather | bytes 835584 | tf_op jit(solution)/shard_map/all_gather | solution.py:33
  528.2 5.2 copy.7
  533.5 7.2 %all-to-all-start.1 = ((f32[16,768,16]{1,2,0:T(8,128)}), f32[16,768,16]{1,2,0:T(8,128)}, u32[]{:S(2)}, u32[]{:S(2)}) async-start(f32[16,768,16]{1,2,0:T(8,128)} %copy.7), calls=%async_computation.1 | async-start | bytes 1572864 | tf_op jit(solution)/shard_map/all_to_all | solution.py:34
  540.7 4.6 fusion.14
  545.3 20.8 %all-to-all-done.1 = f32[16,768,16]{1,2,0:T(8,128)} async-done(((f32[16,768,16]{1,2,0:T(8,128)}), f32[16,768,16]{1,2,0:T(8,128)}, u32[]{:S(2)}, u32[]{:S(2)}) %all-to-all-start.1) | async-done | bytes 786464 | tf_op jit(solution)/shard_map/all_to_all | solution.py:34
  566.0 5.7 fusion.6
Async XLA Ops:
  7.4 54.9 %all-gather.5.cloned.1.call-start = ((), (), s32[]{:S(2)}) async-start(), calls=%async_computation.3 | async-start | bytes 7520256 | tf_op jit(solution)/shard_map/all_gather | solution.py:33
  10.1 0.8 copy-start
  69.0 199.0 %all-to-all-start = ((f32[16,768,144]{1,2,0:T(8,128)}), f32[16,768,144]{1,2,0:T(8,128)}, u32[]{:S(2)}, u32[]{:S(2)}) async-start(f32[16,768,144]{1,2,0:T(8,128)} %bitcast.25), calls=%async_computation | async-start | bytes 14155776 | tf_op jit(solution)/shard_map/all_to_all | solution.py:34
  78.6 224.2 %all-gather.3.cloned.1.call-start = ((), (), s32[]{:S(2)}) async-start(), calls=%async_computation.2 | async-start | bytes 7520256 | tf_op jit(solution)/shard_map/all_gather | solution.py:43
  79.1 404.3 %all-reduce.2.cloned.1.call-start = ((), (), s32[]{:S(2)}) async-start(), calls=%async_computation.4 | async-start | bytes 1572864 | tf_op jit(solution)/shard_map/psum | solution.py:48
  302.8 10.9 %copy-start.1 = (f32[768,768]{1,0:T(8,128)S(1)}, f32[768,768]{1,0:T(8,128)}, u32[]{:S(2)}) copy-start(f32[768,768]{1,0:T(8,128)} %param.4) | copy-start | bytes 7077892
  533.5 32.6 %all-to-all-start.1 = ((f32[16,768,16]{1,2,0:T(8,128)}), f32[16,768,16]{1,2,0:T(8,128)}, u32[]{:S(2)}, u32[]{:S(2)}) async-start(f32[16,768,16]{1,2,0:T(8,128)} %copy.7), calls=%async_computation.1 | async-start | bytes 1572864 | tf_op jit(solution)/shard_map/all_to_all | solution.py:34
Sparse Core Ops, SparseCore 0:
  11.0 51.2 all-gather.4
Sparse Core Ops, SparseCore 1:
  81.6 221.1 all-gather.2
  327.8 155.6 all-reduce.1
where the time goes:
time: 580 us; the launch traced here: 579 us
  waiting for transfers between devices  451 us (78%)
  blocking collectives  43.6 us (8%)
  matrix products  35.2 us (6%)
  local copies, waits for them, and re-layouts  17.7 us (3%)
  starting transfers between devices  16.8 us (3%)
  between operations  14.9 us (3%)
    all_to_all x2, waiting for transfers between devices, column_rows(): lax.all_to_all(gathered, 'col', split_axis=0, concat_axis=1, tiled=True)  210 us
    psum x1, waiting for transfers between devices, local(): image_rows = lax.psum(product(reduced, col_refl), 'col')  156 us
    all_gather x1, waiting for transfers between devices, column_rows(): gathered = lax.all_gather(share, 'row', axis=0, tiled=True)  51.5 us
    all_gather x1, blocking collectives, column_rows(): gathered = lax.all_gather(share, 'row', axis=0, tiled=True)  43.6 us
    all_gather x1, waiting for transfers between devices, local(): row_joined = lax.all_gather(joined, 'col', axis=1, tiled=True)  33.7 us
    dot_general x4, matrix products, outer_rows(): lax.dot_general(first, second, (((1,), (1,)), ((), ())), precision=lax.Pr...  32.3 us
    all_to_all x2, starting transfers between devices, column_rows(): lax.all_to_all(gathered, 'col', split_axis=0, concat_axis=1, tiled=True)  16.7 us
    all_to_all x2, local copies, waits for them, and re-layouts, column_rows(): lax.all_to_all(gathered, 'col', split_axis=0, concat_axis=1, tiled=True)  11.9 us
  transfers between devices with their start and end apart: 5, of which 5 were waited for; matrix products, arithmetic and copies ran while one was open for 1% of the time, Pallas kernels for 0%

commit v1 on v0

v1 whole, which is shorter than its diff:
```python
import functools

import jax
import jax.numpy as jnp
from jax import lax
from jax.experimental import pallas as pl
from jax.experimental.pallas import tpu as pltpu
from jax.sharding import PartitionSpec as P

F32 = jnp.float32
BF16 = jnp.bfloat16
MESH = pl.DeviceIdType.MESH

ROW_TREE = {
    (0, 0): (("+", (1, 0)), ("-", (-1, 0)), ("x", (0, 1))),
    (1, 0): (("+", (2, 0)),),
    (-1, 0): (("-", (-2, 0)),),
    (0, 1): (("+", (1, 1)), ("-", (-1, 1))),
    (2, 0): (("+", (3, 0)), ("x", (2, 1))),
    (-2, 0): (("-", (-3, 0)), ("x", (-2, 1))),
    (3, 0): (("+", (4, 0)),),
    (-3, 0): (),
    (1, 1): (),
    (-1, 1): (),
    (2, 1): (("+", (3, 1)),),
    (-2, 1): (("-", (-3, 1)),),
    (4, 0): (("x", (4, 1)),),
    (3, 1): (),
    (-3, 1): (),
    (4, 1): (),
}
COL_TREE = {
    (0, 0, 0): (("+", (1, 0, 0)), ("-", (-1, 0, 0)), ("x", (0, 1, 0)), ("c", (0, 0, 1))),
    (1, 0, 0): (("+", (2, 0, 0)), ("c", (1, 0, 1))),
    (-1, 0, 0): (("c", (-1, 0, 1)),),
    (0, 1, 0): (("+", (1, 1, 0)), ("-", (-1, 1, 0)), ("c", (0, 1, 1))),
    (2, 0, 0): (("c", (2, 0, 1)),),
    (1, 1, 0): (("+", (2, 1, 0)), ("c", (1, 1, 1))),
    (-1, 1, 0): (("c", (-1, 1, 1)),),
    (2, 1, 0): (("c", (2, 1, 1)),),
    (0, 0, 1): (),
    (1, 0, 1): (),
    (-1, 0, 1): (),
    (0, 1, 1): (),
    (2, 0, 1): (),
    (1, 1, 1): (),
    (-1, 1, 1): (),
    (2, 1, 1): (),
}
ROW_SLOTS = tuple(ROW_TREE)
COL_SLOTS = tuple(COL_TREE)
ROW_ID = {slot: n for n, slot in enumerate(ROW_SLOTS)}
COL_ID = {slot: n for n, slot in enumerate(COL_SLOTS)}


def halves(x):
    high = x.astype(BF16)
    return high, (x - high.astype(F32)).astype(BF16)


def dot(a, b, dims):
    return lax.dot_general(a, b, (dims, ((), ())), preferred_element_type=F32)


NT = ((1,), (1,))
NN = ((1,), (0,))


class Place:
    def __init__(self):
        self.i = lax.axis_index("row")
        self.c = lax.axis_index("col")
        self.core = lax.rem(self.i, 2)
        self.y = lax.rem(self.i // 2, 4)
        self.lo = self.i // 8
        self.z = self.c // 2
        self.hi = lax.rem(self.c, 2)
        self.sign = 1 - 2 * self.core

    def row_share(self, slot):
        d, l = slot
        z = lax.rem(self.z - self.sign * d + 8, 8)
        hi = self.hi if l == 0 else 1 - self.hi
        return z * 2 + hi

    def row_target(self, way):
        if way == "x":
            return (self.i, self.z * 2 + 1 - self.hi)
        step = self.sign if way == "+" else -self.sign
        return (self.i, lax.rem(self.z + step + 8, 8) * 2 + self.hi)

    def col_share(self, slot):
        d, l, s = slot
        sign = self.sign if s == 0 else -self.sign
        y = lax.rem(self.y - sign * d + 4, 4)
        lo = self.lo if l == 0 else 1 - self.lo
        core = self.core if s == 0 else 1 - self.core
        return (lo * 4 + y) * 2 + core

    def col_target(self, way):
        if way == "x":
            return (((1 - self.lo) * 4 + self.y) * 2 + self.core, self.c)
        if way == "c":
            return ((self.lo * 4 + self.y) * 2 + 1 - self.core, self.c)
        step = self.sign if way == "+" else -self.sign
        return ((self.lo * 4 + lax.rem(self.y + step + 4, 4)) * 2 + self.core, self.c)


class Gather:
    def __init__(self, place, kind, buf, send, recv, pieces, own):
        self.kind, self.buf, self.send, self.recv = kind, buf, send, recv
        self.pieces, self.own = pieces, own
        self.tree = ROW_TREE if kind == "row" else COL_TREE
        self.ids = ROW_ID if kind == "row" else COL_ID
        self.share = place.row_share if kind == "row" else place.col_share
        self.target = place.row_target if kind == "row" else place.col_target
        self.depth = buf.shape[1] // pieces

    def copy(self, share, way, child, piece, source):
        rows = pl.ds(piece * self.depth, self.depth)
        n = self.ids[child]
        return pltpu.make_async_remote_copy(
            src_ref=source.at[rows],
            dst_ref=self.buf.at[share, rows],
            send_sem=self.send.at[n, piece],
            recv_sem=self.recv.at[n, piece],
            device_id=self.target(way),
            device_id_type=MESH,
        )

    def start(self, slot, piece, ways=None, source=None):
        share = self.share(slot)
        source = self.buf.at[share] if source is None else source
        for way, child in self.tree[slot]:
            if ways is None or way in ways:
                self.copy(share, way, child, piece, source).start()

    def arrive(self, slot, piece):
        rows = pl.ds(piece * self.depth, self.depth)
        part = self.buf.at[self.share(slot), rows]
        n = self.ids[slot]
        pltpu.make_async_copy(part, part, self.recv.at[n, piece]).wait()

    def drain(self):
        root = next(iter(self.tree))
        for slot, n in self.ids.items():
            if slot == root:
                continue
            for piece in range(self.pieces):
                rows = pl.ds(piece * self.depth, self.depth)
                part = self.buf.at[0, rows]
                pltpu.make_async_copy(part, part, self.send.at[n, piece]).wait()


PIECES = 2


def gather_kernel(
    p_ref, q_ref, v_ref, m_ref,
    red, vrow, vcol, wrow, wcol,
    prow, qcol, lhs, rhs, part_row, part_col, got_row, got_col,
    s_p, r_p, s_q, r_q, s_vr, r_vr, s_vc, r_vc, s_wr, r_wr, s_wc, r_wc,
    s_perm, r_perm, s_sum, r_sum,
):
    at = Place()
    i, c = at.i, at.c
    size = m_ref.shape[0]
    tile = 256

    barrier = pltpu.get_barrier_semaphore()
    for n in range(1, 16):
        other = lax.rem(c + n, 16)
        pl.semaphore_signal(barrier, inc=1, device_id=(i, other), device_id_type=MESH)
        other = lax.rem(i + n, 16)
        pl.semaphore_signal(barrier, inc=1, device_id=(other, c), device_id_type=MESH)

    @pl.when(i != c)
    def _():
        pl.semaphore_signal(barrier, inc=1, device_id=(c, i), device_id_type=MESH)
        pl.semaphore_wait(barrier, 31)

    @pl.when(i == c)
    def _():
        pl.semaphore_wait(barrier, 30)

    g_p = Gather(at, "row", prow, s_p, r_p, PIECES, p_ref)
    g_q = Gather(at, "col", qcol, s_q, r_q, PIECES, q_ref)
    g_vr = Gather(at, "row", vrow, s_vr, r_vr, 1, v_ref)
    g_vc = Gather(at, "col", vcol, s_vc, r_vc, 1, v_ref)
    g_wr = Gather(at, "row", wrow, s_wr, r_wr, 1, None)
    g_wc = Gather(at, "col", wcol, s_wc, r_wc, 1, None)

    def crossing(gather, piece, n):
        rows = pl.ds(piece * gather.depth, gather.depth)
        return pltpu.make_async_remote_copy(
            src_ref=gather.own.at[rows],
            dst_ref=gather.buf.at[c, rows],
            send_sem=s_perm.at[n],
            recv_sem=r_perm.at[n],
            device_id=(c, i),
            device_id_type=MESH,
        )

    crossings = [(g_vc, 0, 0)] + [(g_q, piece, 1 + piece) for piece in range(PIECES)]

    g_vr.start((0, 0), 0, source=v_ref)

    @pl.when(i != c)
    def _():
        for args in crossings:
            crossing(*args).start()

    for piece in range(PIECES):
        g_p.start((0, 0), piece, source=p_ref)

    vrow[c] = v_ref[...]
    prow[c] = p_ref[...]

    @pl.when(i == c)
    def _():
        g_vc.start((0, 0, 0), 0, source=v_ref)
        for piece in range(PIECES):
            g_q.start((0, 0, 0), piece, source=q_ref)
        vcol[i] = v_ref[...]
        qcol[i] = q_ref[...]

    def crossed(gather, piece, n):
        @pl.when(i != c)
        def _():
            rows = pl.ds(piece * gather.depth, gather.depth)
            part = gather.buf.at[i, rows]
            pltpu.make_async_copy(part, part, r_perm.at[n]).wait()
            gather.start((0, 0, 0), piece)

    def row_step(gather, slot):
        for piece in range(gather.pieces):
            gather.arrive(slot, piece)
            gather.start(slot, piece)

    def col_step(gather, slot):
        for piece in range(gather.pieces):
            gather.arrive(slot, piece)
            gather.start(slot, piece)

    red[...] = m_ref[...]

    def accumulate(first, second):
        k1, k2 = at.row_share(first), at.row_share(second)
        for n, k in enumerate((k1, k2)):
            high, low = halves(prow[k])
            lhs[:, pl.ds(n * 128, 128)] = high
            lhs[:, pl.ds(256 + n * 128, 128)] = low
            lhs[:, pl.ds(512 + n * 128, 128)] = high
            high, low = halves(qcol[k])
            rhs[:, pl.ds(n * 128, 128)] = high
            rhs[:, pl.ds(256 + n * 128, 128)] = high
            rhs[:, pl.ds(512 + n * 128, 128)] = low

        @pl.loop(0, size // tile)
        def _(t):
            rows = pl.ds(pl.multiple_of(t * tile, tile), tile)
            red[rows, :] += dot(lhs[rows, :], rhs[...], NT)

    for args in crossings:
        crossed(*args)
    for slot in ((0, 1), (1, 0), (-1, 0)):
        row_step(g_vr, slot)
        row_step(g_p, slot)
    for slot in ((0, 0, 1), (1, 0, 0), (-1, 0, 0), (0, 1, 0)):
        col_step(g_vc, slot)
        col_step(g_q, slot)
    for slot in ((2, 0), (-2, 0)):
        row_step(g_vr, slot)
        row_step(g_p, slot)
    for slot in ((2, 0, 0), (1, 1, 0)):
        col_step(g_vc, slot)
        col_step(g_q, slot)
    for slot in ((1, 1), (-1, 1), (3, 0), (-3, 0)):
        row_step(g_vr, slot)
        row_step(g_p, slot)
    for slot in ((-1, 1, 0), (2, 1, 0)):
        col_step(g_vc, slot)
        col_step(g_q, slot)
    for slot in ((2, 1), (-2, 1)):
        row_step(g_vr, slot)
        row_step(g_p, slot)
    for slot in ((1, 0, 1), (-1, 0, 1), (0, 1, 1), (2, 0, 1), (1, 1, 1), (-1, 1, 1), (2, 1, 1)):
        col_step(g_vc, slot)
        col_step(g_q, slot)
    accumulate((0, 0), (0, 1))
    accumulate((1, 0), (-1, 0))
    row_step(g_vr, (4, 0))
    row_step(g_p, (4, 0))
    accumulate((2, 0), (-2, 0))
    accumulate((1, 1), (-1, 1))
    accumulate((3, 0), (-3, 0))
    accumulate((2, 1), (-2, 1))
    for slot in ((3, 1), (-3, 1)):
        row_step(g_vr, slot)
        row_step(g_p, slot)
    accumulate((3, 1), (-3, 1))
    for slot in ((4, 1),):
        row_step(g_vr, slot)
        row_step(g_p, slot)
    accumulate((4, 0), (4, 1))

    high, low = halves(red[...])
    lhs[...] = high
    rhs[...] = low
    width = v_ref.shape[0]
    count = 16 * width
    vh, vl = halves(vcol[...].reshape(count, size))
    part_row[...] = (
        dot(vh, lhs[...], NT) + dot(vh, rhs[...], NT) + dot(vl, lhs[...], NT)
    ).reshape(16, width, size)

    def addend(buf, got, share, target, n):
        return pltpu.make_async_remote_copy(
            src_ref=buf.at[share],
            dst_ref=got.at[n],
            send_sem=s_sum.at[n + (15 if got is got_col else 0)],
            recv_sem=r_sum.at[n + (15 if got is got_col else 0)],
            device_id=target,
            device_id_type=MESH,
        )

    order = (8, 7, 9, 6, 10, 5, 11, 4, 12, 3, 13, 2, 14, 1, 15)
    for n in order:
        other = lax.rem(c + n, 16)
        addend(part_row, got_row, other, (i, other), n - 1).start()
    vh, vl = halves(vrow[...].reshape(count, size))
    part_col[...] = -(
        dot(vh, lhs[...], NN) + dot(vh, rhs[...], NN) + dot(vl, lhs[...], NN)
    ).reshape(16, width, size)
    for n in order:
        other = lax.rem(i + n, 16)
        addend(part_col, got_col, other, (other, c), n - 1).start()

    def gathered(got, n, sem):
        pltpu.make_async_copy(got.at[n], got.at[n], r_sum.at[sem]).wait()

    total = part_col[i]
    for n in range(15):
        gathered(got_col, n, n + 15)
        total += got_col[n]
    wcol[i] = total
    g_wc.start((0, 0, 0), 0)
    total = part_row[c]
    for n in range(15):
        gathered(got_row, n, n)
        total += got_row[n]
    wrow[c] = total
    g_wr.start((0, 0), 0)

    for slot in ((1, 0, 0), (-1, 0, 0), (0, 1, 0)):
        col_step(g_wc, slot)
    for slot in ((1, 0), (-1, 0), (0, 1)):
        row_step(g_wr, slot)
    for slot in ((2, 0, 0), (1, 1, 0), (-1, 1, 0)):
        col_step(g_wc, slot)
    for slot in ((2, 0), (-2, 0), (1, 1), (-1, 1)):
        row_step(g_wr, slot)
    col_step(g_wc, (2, 1, 0))
    for slot in ((3, 0), (-3, 0), (2, 1), (-2, 1)):
        row_step(g_wr, slot)
    for slot in COL_SLOTS[8:]:
        col_step(g_wc, slot)
    for slot in ((4, 0), (3, 1), (-3, 1), (4, 1)):
        row_step(g_wr, slot)

    for gather in (g_p, g_q, g_vr, g_vc, g_wr, g_wc):
        gather.drain()

    @pl.when(i != c)
    def _():
        for gather, piece, n in crossings:
            rows = pl.ds(piece * gather.depth, gather.depth)
            part = gather.own.at[rows]
            pltpu.make_async_copy(part, part, s_perm.at[n]).wait()

    for n in range(30):
        pltpu.make_async_copy(got_row.at[0], got_row.at[0], s_sum.at[n]).wait()


def update_kernel(red, vrow, wrow, vcol, wcol, out, lhs):
    count, size = vrow.shape

    @pl.when(pl.program_id(0) == 0)
    def _():
        for n, ref in enumerate((vrow, wrow)):
            high, low = halves(ref[...].T)
            lhs[:, pl.ds(n * count, count)] = high
            lhs[:, pl.ds((2 + n) * count, count)] = low

    wh, wl = halves(wcol[...])
    vh, vl = halves(-vcol[...])
    high = jnp.concatenate([wh, vh], axis=0)
    low = jnp.concatenate([wl, vl], axis=0)
    first = lhs[:, : 2 * count]
    out[...] = red[...] + (
        dot(first, high, NN) + dot(first, low, NN) + dot(lhs[:, 2 * count :], high, NN)
    )


def local(matrix, left_panel, right_panel, reflectors):
    size = matrix.shape[0]
    width = reflectors.shape[1]
    count = 16 * width
    panel = jnp.concatenate([left_panel, right_panel], axis=1)
    swapped = jnp.concatenate([-right_panel, left_panel], axis=1)
    flat = reflectors.T
    vmem = pl.BlockSpec(memory_space=pltpu.VMEM)
    dma = pltpu.SemaphoreType.DMA
    small = jax.ShapeDtypeStruct((16, width, size), F32)
    sems = [dma((16, PIECES))] * 4 + [dma((16, 1))] * 8 + [dma((1 + PIECES,))] * 2 + [dma((30,))] * 2
    red, vrow, vcol, wrow, wcol = pl.pallas_call(
        gather_kernel,
        name="gather",
        out_shape=(jax.ShapeDtypeStruct((size, size), F32), small, small, small, small),
        in_specs=[vmem] * 4,
        out_specs=(vmem,) * 5,
        scratch_shapes=[
            pltpu.VMEM((16, size, 128), F32),
            pltpu.VMEM((16, size, 128), F32),
            pltpu.VMEM((size, size), BF16),
            pltpu.VMEM((size, size), BF16),
            pltpu.VMEM((16, width, size), F32),
            pltpu.VMEM((16, width, size), F32),
            pltpu.VMEM((15, width, size), F32),
            pltpu.VMEM((15, width, size), F32),
        ]
        + sems,
        compiler_params=pltpu.CompilerParams(
            collective_id=0, has_side_effects=True, vmem_limit_bytes=56 * 1024 * 1024
        ),
    )(panel, swapped, flat, matrix)
    vrow, vcol, wrow, wcol = (x.reshape(count, size) for x in (vrow, vcol, wrow, wcol))
    tile = 256
    whole = pl.BlockSpec((count, size), lambda n: (0, 0))
    strip = pl.BlockSpec((count, tile), lambda n: (0, n))
    block = pl.BlockSpec((size, tile), lambda n: (0, n))
    return pl.pallas_call(
        update_kernel,
        name="update",
        grid=(size // tile,),
        out_shape=jax.ShapeDtypeStruct((size, size), F32),
        in_specs=[block, whole, whole, strip, strip],
        out_specs=block,
        scratch_shapes=[pltpu.VMEM((size, 4 * count), BF16)],
        compiler_params=pltpu.CompilerParams(dimension_semantics=("arbitrary",)),
    )(red, vrow, wrow, vcol, wcol)


def solution(mesh):
    in_specs = (P("row", "col"), P("row", "col"), P("row", "col"), P("row", "col"))
    out_specs = P("row", "col")
    return jax.shard_map(local, mesh=mesh, in_specs=in_specs, out_specs=out_specs, check_vma=False)
```

time: 580 us -> 171 us (0.29)
  waiting for transfers between devices: 451 us -> 0 us
  Pallas kernels: 0 us -> 165 us
  blocking collectives: 43.6 us -> 0 us
  matrix products: 35.2 us -> 0 us
  starting transfers between devices: 16.8 us -> 0 us
  local copies, waits for them, and re-layouts: 17.7 us -> 2.36 us
  between operations: 14.9 us -> 0.02 us
    all_to_all x2 -> x0, waiting for transfers between devices: 210 us -> none  [column_rows(): lax.all_to_all(gathered, 'col', split_axis=0, concat_axis=1, tiled=True)]
    pallas_call x0 -> x2, Pallas kernels: none -> 165 us  [the longest x1 159 us: local(): pl.pallas_call(gather_kernel, name='gather', out_shape=(jax.ShapeDtypeStr...]
    psum x1 -> x0, waiting for transfers between devices: 156 us -> none  [local(): image_rows = lax.psum(product(reduced, col_refl), 'col')]
    all_gather x2 -> x0, waiting for transfers between devices: 85.1 us -> none  [the longest x1 51.5 us: column_rows(): gathered = lax.all_gather(share, 'row', axis=0, tiled=True)]
    all_gather x1 -> x0, blocking collectives: 43.6 us -> none  [column_rows(): gathered = lax.all_gather(share, 'row', axis=0, tiled=True)]
    dot_general x5 -> x0, matrix products: 35.2 us -> none  [the longest x4 32.3 us: outer_rows(): lax.dot_general(first, second, (((1,), (1,)), ((), ())), precision=lax.Pr...]
    all_to_all x2 -> x0, starting transfers between devices: 16.7 us -> none  [column_rows(): lax.all_to_all(gathered, 'col', split_axis=0, concat_axis=1, tiled=True)]
    all_to_all x2 -> x0, local copies, waits for them, and re-layouts: 11.9 us -> none  [column_rows(): lax.all_to_all(gathered, 'col', split_axis=0, concat_axis=1, tiled=True)]
  transfers between devices with their start and end apart: 5 -> 0, of which waited for: 5 -> 0; matrix products, arithmetic and copies ran while one was open for 1% -> 0% of each run, Pallas kernels for 0% -> 0%
where the time goes in v1:
time: 171 us; the launch traced here: 170 us
  Pallas kernels  165 us (96%)
  local copies, waits for them, and re-layouts  2.36 us (1%)
  other arithmetic  2.13 us (1%)
    pallas_call x1, Pallas kernels, local(): pl.pallas_call(gather_kernel, name='gather', out_shape=(jax.ShapeDtypeStr...  159 us
    pallas_call x1, Pallas kernels, local(): pl.pallas_call(update_kernel, name='update', grid=(size // tile,), out_sh...  6.41 us

profile of v1, /device:TPU:8, one launch (start us, length us, event | category | flops | bytes accessed | tf_op | source)
XLA Modules:
  0.0 169.6 jit_solution(15818237142691480279)
XLA Ops:
  0.0 0.9 neg.3
  0.9 0.2 copy.11
  1.1 1.1 copy.9
  2.2 1.1 copy.10
  3.3 1.2 pad_maximum_fusion.1
  4.5 158.7 %gather.1 = (f32[768,768]{1,0:T(8,128)}, f32[16,16,768]{2,1,0:T(8,128)}, f32[16,16,768]{2,1,0:T(8,128)}, f32[16,16,768]{2,1,0:T(8,128)}, f32[16,16,768]{2,1,0:T(8,128)}) custom-call(f32[768,128]{1,0:T(8,128)} %get-tuple-element.16.p_ref, f32[768,128]{1,0:T(8,128)} %get-tuple-element.15.q_ref, f32[16,768]{1,0:T(8,128)} %bitcast.9, f32[768,768]{1,0:T(8,128)} %m_ref.1), custom_call_target="tpu_custom_call" | custom-call | tf_op jit(solution)/shard_map/gather/pallas_call | solution.py:416
  163.2 6.4 %update.1 = f32[768,768]{1,0:T(8,128)} custom-call(f32[768,768]{1,0:T(8,128)} %get-tuple-element.10.red, f32[256,768]{1,0:T(8,128)} %bitcast.5, f32[256,768]{1,0:T(8,128)} %bitcast.7, f32[256,768]{1,0:T(8,128)} %bitcast.6, f32[256,768]{1,0:T(8,128)} %bitcast.8), custom_call_target="tpu_custom_call" | custom-call | tf_op jit(solution)/shard_map/update/pallas_call | solution.py:442

commit v2 on v1

--- a/solution.py
+++ b/solution.py
@@ -47,6 +47,43 @@
     (-1, 1, 1): (),
     (2, 1, 1): (),
 }
+ROW_FLAT = {
+    (0, 0): (("++", (2, 0)), ("--", (-2, 0)), ("+", (1, 0)), ("-", (-1, 0)), ("x", (0, 1))),
+    (1, 0): (("x", (1, 1)),),
+    (-1, 0): (("x", (-1, 1)),),
+    (0, 1): (),
+    (2, 0): (("++", (4, 0)), ("+", (3, 0)), ("x", (2, 1))),
+    (-2, 0): (("-", (-3, 0)), ("x", (-2, 1))),
+    (3, 0): (("x", (3, 1)),),
+    (-3, 0): (("x", (-3, 1)),),
+    (1, 1): (),
+    (-1, 1): (),
+    (2, 1): (),
+    (-2, 1): (),
+    (4, 0): (("x", (4, 1)),),
+    (3, 1): (),
+    (-3, 1): (),
+    (4, 1): (),
+}
+COL_FLAT = {
+    (0, 0, 0): (("++", (2, 0, 0)), ("+", (1, 0, 0)), ("-", (-1, 0, 0)), ("x", (0, 1, 0)), ("c", (0, 0, 1))),
+    (1, 0, 0): (("x", (1, 1, 0)), ("c", (1, 0, 1))),
+    (-1, 0, 0): (("x", (-1, 1, 0)), ("c", (-1, 0, 1))),
+    (0, 1, 0): (("c", (0, 1, 1)),),
+    (2, 0, 0): (("x", (2, 1, 0)), ("c", (2, 0, 1))),
+    (1, 1, 0): (("c", (1, 1, 1)),),
+    (-1, 1, 0): (("c", (-1, 1, 1)),),
+    (2, 1, 0): (("c", (2, 1, 1)),),
+    (0, 0, 1): (),
+    (1, 0, 1): (),
+    (-1, 0, 1): (),
+    (0, 1, 1): (),
+    (2, 0, 1): (),
+    (1, 1, 1): (),
+    (-1, 1, 1): (),
+    (2, 1, 1): (),
+}
+STEPS = {"+": 1, "-": -1, "++": 2, "--": -2}
 ROW_SLOTS = tuple(ROW_TREE)
 COL_SLOTS = tuple(COL_TREE)
 ROW_ID = {slot: n for n, slot in enumerate(ROW_SLOTS)}
@@ -86,7 +123,7 @@
     def row_target(self, way):
         if way == "x":
             return (self.i, self.z * 2 + 1 - self.hi)
-        step = self.sign if way == "+" else -self.sign
+        step = self.sign * STEPS[way]
         return (self.i, lax.rem(self.z + step + 8, 8) * 2 + self.hi)
 
     def col_share(self, slot):
@@ -95,22 +132,27 @@
         y = lax.rem(self.y - sign * d + 4, 4)
         lo = self.lo if l == 0 else 1 - self.lo
         core = self.core if s == 0 else 1 - self.core
-        return (lo * 4 + y) * 2 + core
+        return self.held((lo * 4 + y) * 2 + core, self.c)
+
+    @staticmethod
+    def held(i, c):
+        core = lax.rem(i, 2)
+        return lax.rem(i // 2 - c // 2 - 4 * core + 16, 8) * 2 + core
 
     def col_target(self, way):
         if way == "x":
             return (((1 - self.lo) * 4 + self.y) * 2 + self.core, self.c)
         if way == "c":
             return ((self.lo * 4 + self.y) * 2 + 1 - self.core, self.c)
-        step = self.sign if way == "+" else -self.sign
+        step = self.sign * STEPS[way]
         return ((self.lo * 4 + lax.rem(self.y + step + 4, 4)) * 2 + self.core, self.c)
 
 
 class Gather:
-    def __init__(self, place, kind, buf, send, recv, pieces, own):
+    def __init__(self, place, kind, tree, buf, send, recv, pieces, own):
         self.kind, self.buf, self.send, self.recv = kind, buf, send, recv
         self.pieces, self.own = pieces, own
-        self.tree = ROW_TREE if kind == "row" else COL_TREE
+        self.tree = tree
         self.ids = ROW_ID if kind == "row" else COL_ID
         self.share = place.row_share if kind == "row" else place.col_share
         self.target = place.row_target if kind == "row" else place.col_target
@@ -156,11 +198,11 @@
 
 
 def gather_kernel(
-    p_ref, q_ref, v_ref, m_ref,
+    left_ref, right_ref, v_ref, m_ref,
     red, vrow, vcol, wrow, wcol,
-    prow, qcol, lhs, rhs, part_row, part_col, got_row, got_col,
+    prow, qcol, q_ref, qmid, vmid, lhs, rhs, part_row, part_col, got_row, got_col,
     s_p, r_p, s_q, r_q, s_vr, r_vr, s_vc, r_vc, s_wr, r_wr, s_wc, r_wc,
-    s_perm, r_perm, s_sum, r_sum,
+    s_one, r_one, s_two, r_two, s_sum, r_sum,
 ):
     at = Place()
     i, c = at.i, at.c
@@ -174,63 +216,106 @@
         other = lax.rem(i + n, 16)
         pl.semaphore_signal(barrier, inc=1, device_id=(other, c), device_id_type=MESH)
 
-    @pl.when(i != c)
-    def _():
-        pl.semaphore_signal(barrier, inc=1, device_id=(c, i), device_id_type=MESH)
-        pl.semaphore_wait(barrier, 31)
-
-    @pl.when(i == c)
-    def _():
+    held = at.held(i, c)
+    middle = (lax.rem(at.z + i // 2 + 4 * at.hi, 8) * 2 + at.hi, at.z * 2 + at.core)
+    opposite = held // 2
+    source = (opposite * 2 + at.hi, at.z * 2 + at.core)
+    beyond = (i, opposite * 2 + at.hi)
+    moves = jnp.logical_or(at.core != at.hi, lax.rem(at.z + 4 * at.hi, 8) != 0)
+    stays = opposite == at.z
+
+    @pl.when(moves)
+    def _():
+        pl.semaphore_signal(barrier, inc=1, device_id=middle, device_id_type=MESH)
+        pl.semaphore_signal(barrier, inc=1, device_id=source, device_id_type=MESH)
+
+    left, right = left_ref[...], right_ref[...]
+    q_ref[...] = jnp.concatenate([-right, left], axis=0).T
+    prow[c] = jnp.concatenate([left, right], axis=0).T
+    vrow[c] = v_ref[...]
+    red[...] = m_ref[...]
+
+    @pl.when(moves)
+    def _():
+        pl.semaphore_wait(barrier, 32)
+
+    @pl.when(jnp.logical_not(moves))
+    def _():
+        qmid[...] = q_ref[...]
+        vmid[...] = v_ref[...]
         pl.semaphore_wait(barrier, 30)
 
-    g_p = Gather(at, "row", prow, s_p, r_p, PIECES, p_ref)
-    g_q = Gather(at, "col", qcol, s_q, r_q, PIECES, q_ref)
-    g_vr = Gather(at, "row", vrow, s_vr, r_vr, 1, v_ref)
-    g_vc = Gather(at, "col", vcol, s_vc, r_vc, 1, v_ref)
-    g_wr = Gather(at, "row", wrow, s_wr, r_wr, 1, None)
-    g_wc = Gather(at, "col", wcol, s_wc, r_wc, 1, None)
-
-    def crossing(gather, piece, n):
+    @pl.when(jnp.logical_and(jnp.logical_not(moves), stays))
+    def _():
+        qcol[held] = q_ref[...]
+        vcol[held] = v_ref[...]
+
+    g_p = Gather(at, "row", ROW_TREE, prow, s_p, r_p, PIECES, None)
+    g_q = Gather(at, "col", COL_TREE, qcol, s_q, r_q, PIECES, q_ref)
+    g_vr = Gather(at, "row", ROW_FLAT, vrow, s_vr, r_vr, 1, v_ref)
+    g_vc = Gather(at, "col", COL_FLAT, vcol, s_vc, r_vc, 1, v_ref)
+    g_wr = Gather(at, "row", ROW_FLAT, wrow, s_wr, r_wr, 1, None)
+    g_wc = Gather(at, "col", COL_FLAT, wcol, s_wc, r_wc, 1, None)
+
+    crossings = ((g_vc, v_ref, vmid, 0, 0),) + tuple((g_q, q_ref, qmid, n, 1 + n) for n in range(PIECES))
+
+    def first_copy(gather, own, mid, piece, n, direct):
         rows = pl.ds(piece * gather.depth, gather.depth)
         return pltpu.make_async_remote_copy(
-            src_ref=gather.own.at[rows],
-            dst_ref=gather.buf.at[c, rows],
-            send_sem=s_perm.at[n],
-            recv_sem=r_perm.at[n],
-            device_id=(c, i),
+            src_ref=own.at[rows],
+            dst_ref=gather.buf.at[c, rows] if direct else mid.at[rows],
+            send_sem=s_one.at[n],
+            recv_sem=r_one.at[n],
+            device_id=middle,
             device_id_type=MESH,
         )
 
-    crossings = [(g_vc, 0, 0)] + [(g_q, piece, 1 + piece) for piece in range(PIECES)]
-
-    g_vr.start((0, 0), 0, source=v_ref)
-
-    @pl.when(i != c)
+    def second_copy(gather, own, mid, piece, n):
+        rows = pl.ds(piece * gather.depth, gather.depth)
+        return pltpu.make_async_remote_copy(
+            src_ref=mid.at[rows],
+            dst_ref=gather.buf.at[at.z * 2 + at.core, rows],
+            send_sem=s_two.at[n],
+            recv_sem=r_two.at[n],
+            device_id=beyond,
+            device_id_type=MESH,
+        )
+
+    g_vr.start((0, 0), 0)
+
+    @pl.when(jnp.logical_and(moves, i // 2 == at.z))
     def _():
         for args in crossings:
-            crossing(*args).start()
+            first_copy(*args, True).start()
+
+    @pl.when(jnp.logical_and(moves, i // 2 != at.z))
+    def _():
+        for args in crossings:
+            first_copy(*args, False).start()
 
     for piece in range(PIECES):
-        g_p.start((0, 0), piece, source=p_ref)
-
-    vrow[c] = v_ref[...]
-    prow[c] = p_ref[...]
-
-    @pl.when(i == c)
-    def _():
-        g_vc.start((0, 0, 0), 0, source=v_ref)
-        for piece in range(PIECES):
-            g_q.start((0, 0, 0), piece, source=q_ref)
-        vcol[i] = v_ref[...]
-        qcol[i] = q_ref[...]
-
-    def crossed(gather, piece, n):
-        @pl.when(i != c)
+        g_p.start((0, 0), piece)
+
+    def relay(gather, own, mid, piece, n):
+        rows = pl.ds(piece * gather.depth, gather.depth)
+
+        @pl.when(moves)
         def _():
-            rows = pl.ds(piece * gather.depth, gather.depth)
-            part = gather.buf.at[i, rows]
-            pltpu.make_async_copy(part, part, r_perm.at[n]).wait()
-            gather.start((0, 0, 0), piece)
+            pltpu.make_async_copy(mid.at[rows], mid.at[rows], r_one.at[n]).wait()
+
+        @pl.when(jnp.logical_not(stays))
+        def _():
+            second_copy(gather, own, mid, piece, n).start()
+
+    def crossed(gather, own, mid, piece, n):
+        rows = pl.ds(piece * gather.depth, gather.depth)
+
+        @pl.when(jnp.logical_not(stays))
+        def _():
+            part = gather.buf.at[held, rows]
+            pltpu.make_async_copy(part, part, r_two.at[n]).wait()
+
+        gather.start((0, 0, 0), piece)
 
     def row_step(gather, slot):
         for piece in range(gather.pieces):
@@ -241,8 +326,6 @@
         for piece in range(gather.pieces):
             gather.arrive(slot, piece)
             gather.start(slot, piece)
-
-    red[...] = m_ref[...]
 
     def accumulate(first, second):
         k1, k2 = at.row_share(first), at.row_share(second)
@@ -261,36 +344,38 @@
             rows = pl.ds(pl.multiple_of(t * tile, tile), tile)
             red[rows, :] += dot(lhs[rows, :], rhs[...], NT)
 
+    row_step(g_vr, (1, 0))
+    row_step(g_vr, (-1, 0))
+    for args in crossings:
+        relay(*args)
+    for slot in ((0, 1), (1, 0), (-1, 0)):
+        row_step(g_p, slot)
     for args in crossings:
         crossed(*args)
-    for slot in ((0, 1), (1, 0), (-1, 0)):
+    for slot in ((2, 0), (-2, 0)):
         row_step(g_vr, slot)
         row_step(g_p, slot)
+    row_step(g_vr, (0, 1))
     for slot in ((0, 0, 1), (1, 0, 0), (-1, 0, 0), (0, 1, 0)):
         col_step(g_vc, slot)
         col_step(g_q, slot)
-    for slot in ((2, 0), (-2, 0)):
+    for slot in ((3, 0), (-3, 0), (1, 1), (-1, 1)):
         row_step(g_vr, slot)
         row_step(g_p, slot)
     for slot in ((2, 0, 0), (1, 1, 0)):
         col_step(g_vc, slot)
         col_step(g_q, slot)
-    for slot in ((1, 1), (-1, 1), (3, 0), (-3, 0)):
+    for slot in ((2, 1), (-2, 1), (4, 0)):
         row_step(g_vr, slot)
         row_step(g_p, slot)
     for slot in ((-1, 1, 0), (2, 1, 0)):
         col_step(g_vc, slot)
         col_step(g_q, slot)
-    for slot in ((2, 1), (-2, 1)):
-        row_step(g_vr, slot)
-        row_step(g_p, slot)
     for slot in ((1, 0, 1), (-1, 0, 1), (0, 1, 1), (2, 0, 1), (1, 1, 1), (-1, 1, 1), (2, 1, 1)):
         col_step(g_vc, slot)
         col_step(g_q, slot)
     accumulate((0, 0), (0, 1))
     accumulate((1, 0), (-1, 0))
-    row_step(g_vr, (4, 0))
-    row_step(g_p, (4, 0))
     accumulate((2, 0), (-2, 0))
     accumulate((1, 1), (-1, 1))
     accumulate((3, 0), (-3, 0))
@@ -334,16 +419,16 @@
     ).reshape(16, width, size)
     for n in order:
         other = lax.rem(i + n, 16)
-        addend(part_col, got_col, other, (other, c), n - 1).start()
+        addend(part_col, got_col, at.held(other, c), (other, c), n - 1).start()
 
     def gathered(got, n, sem):
         pltpu.make_async_copy(got.at[n], got.at[n], r_sum.at[sem]).wait()
 
-    total = part_col[i]
+    total = part_col[held]
     for n in range(15):
         gathered(got_col, n, n + 15)
         total += got_col[n]
-    wcol[i] = total
+    wcol[held] = total
     g_wc.start((0, 0, 0), 0)
     total = part_row[c]
     for n in range(15):
@@ -352,31 +437,33 @@
     wrow[c] = total
     g_wr.start((0, 0), 0)
 
-    for slot in ((1, 0, 0), (-1, 0, 0), (0, 1, 0)):
+    for slot in ((0, 0, 1), (1, 0, 0), (-1, 0, 0), (2, 0, 0), (0, 1, 0)):
         col_step(g_wc, slot)
-    for slot in ((1, 0), (-1, 0), (0, 1)):
+    for slot in ((1, 0), (-1, 0), (2, 0), (-2, 0), (0, 1)):
         row_step(g_wr, slot)
-    for slot in ((2, 0, 0), (1, 1, 0), (-1, 1, 0)):
+    for slot in ((1, 1, 0), (-1, 1, 0), (2, 1, 0)):
         col_step(g_wc, slot)
-    for slot in ((2, 0), (-2, 0), (1, 1), (-1, 1)):
+    for slot in ((3, 0), (-3, 0), (4, 0), (1, 1), (-1, 1), (2, 1), (-2, 1)):
         row_step(g_wr, slot)
-    col_step(g_wc, (2, 1, 0))
-    for slot in ((3, 0), (-3, 0), (2, 1), (-2, 1)):
-        row_step(g_wr, slot)
-    for slot in COL_SLOTS[8:]:
+    for slot in COL_SLOTS[9:]:
         col_step(g_wc, slot)
-    for slot in ((4, 0), (3, 1), (-3, 1), (4, 1)):
+    for slot in ((3, 1), (-3, 1), (4, 1)):
         row_step(g_wr, slot)
 
     for gather in (g_p, g_q, g_vr, g_vc, g_wr, g_wc):
         gather.drain()
 
-    @pl.when(i != c)
-    def _():
-        for gather, piece, n in crossings:
-            rows = pl.ds(piece * gather.depth, gather.depth)
-            part = gather.own.at[rows]
-            pltpu.make_async_copy(part, part, s_perm.at[n]).wait()
+    @pl.when(moves)
+    def _():
+        for gather, own, mid, piece, n in crossings:
+            part = own.at[pl.ds(piece * gather.depth, gather.depth)]
+            pltpu.make_async_copy(part, part, s_one.at[n]).wait()
+
+    @pl.when(jnp.logical_not(stays))
+    def _():
+        for gather, own, mid, piece, n in crossings:
+            part = mid.at[pl.ds(piece * gather.depth, gather.depth)]
+            pltpu.make_async_copy(part, part, s_two.at[n]).wait()
 
     for n in range(30):
         pltpu.make_async_copy(got_row.at[0], got_row.at[0], s_sum.at[n]).wait()
@@ -406,13 +493,10 @@
     size = matrix.shape[0]
     width = reflectors.shape[1]
     count = 16 * width
-    panel = jnp.concatenate([left_panel, right_panel], axis=1)
-    swapped = jnp.concatenate([-right_panel, left_panel], axis=1)
-    flat = reflectors.T
     vmem = pl.BlockSpec(memory_space=pltpu.VMEM)
     dma = pltpu.SemaphoreType.DMA
     small = jax.ShapeDtypeStruct((16, width, size), F32)
-    sems = [dma((16, PIECES))] * 4 + [dma((16, 1))] * 8 + [dma((1 + PIECES,))] * 2 + [dma((30,))] * 2
+    sems = [dma((16, PIECES))] * 4 + [dma((16, 1))] * 8 + [dma((1 + PIECES,))] * 4 + [dma((30,))] * 2
     red, vrow, vcol, wrow, wcol = pl.pallas_call(
         gather_kernel,
         name="gather",
@@ -422,6 +506,9 @@
         scratch_shapes=[
             pltpu.VMEM((16, size, 128), F32),
             pltpu.VMEM((16, size, 128), F32),
+            pltpu.VMEM((size, 128), F32),
+            pltpu.VMEM((size, 128), F32),
+            pltpu.VMEM((width, size), F32),
             pltpu.VMEM((size, size), BF16),
             pltpu.VMEM((size, size), BF16),
             pltpu.VMEM((16, width, size), F32),
@@ -433,7 +520,7 @@
         compiler_params=pltpu.CompilerParams(
             collective_id=0, has_side_effects=True, vmem_limit_bytes=56 * 1024 * 1024
         ),
-    )(panel, swapped, flat, matrix)
+    )(left_panel.T, right_panel.T, reflectors.T, matrix)
     vrow, vcol, wrow, wcol = (x.reshape(count, size) for x in (vrow, vcol, wrow, wcol))
     tile = 256
     whole = pl.BlockSpec((count, size), lambda n: (0, 0))

time: 171 us -> 148 us (0.87)
  Pallas kernels: 165 us -> 145 us
  local copies, waits for them, and re-layouts: 2.36 us -> 0 us
  other arithmetic: 2.13 us -> 0 us
    pallas_call x1, Pallas kernels: 159 us -> 139 us  [local(): pl.pallas_call(gather_kernel, name='gather', out_shape=(jax.ShapeDtypeStr...]
    unnamed x2 -> x0, local copies, waits for them, and re-layouts: 2.19 us -> none
where the time goes in v2:
time: 148 us; the launch traced here: 145 us
  Pallas kernels  145 us (98%)
    pallas_call x1, Pallas kernels, local(): pl.pallas_call(gather_kernel, name='gather', out_shape=(jax.ShapeDtypeStr...  139 us
    pallas_call x1, Pallas kernels, local(): pl.pallas_call(update_kernel, name='update', grid=(size // tile,), out_sh...  6.4 us

profile of v2, /device:TPU:8, one launch (start us, length us, event | category | flops | bytes accessed | tf_op | source)
XLA Modules:
  0.0 145.3 jit_solution(4447935053435055789)
XLA Ops:
  0.0 138.9 %gather.1 = (f32[768,768]{1,0:T(8,128)}, f32[16,16,768]{2,1,0:T(8,128)}, f32[16,16,768]{2,1,0:T(8,128)}, f32[16,16,768]{2,1,0:T(8,128)}, f32[16,16,768]{2,1,0:T(8,128)}) custom-call(f32[64,768]{1,0:T(8,128)} %bitcast.11, f32[64,768]{1,0:T(8,128)} %bitcast.12, f32[16,768]{1,0:T(8,128)} %bitcast.13, f32[768,768]{1,0:T(8,128)} %m_ref.1), custom_call_target="tpu_custom_call" | custom-call | tf_op jit(solution)/shard_map/gather/pallas_call | solution.py:500
  138.9 6.4 %update.1 = f32[768,768]{1,0:T(8,128)} custom-call(f32[768,768]{1,0:T(8,128)} %get-tuple-element.10.red, f32[256,768]{1,0:T(8,128)} %bitcast.7, f32[256,768]{1,0:T(8,128)} %bitcast.9, f32[256,768]{1,0:T(8,128)} %bitcast.8, f32[256,768]{1,0:T(8,128)} %bitcast.10), custom_call_target="tpu_custom_call" | custom-call | tf_op jit(solution)/shard_map/update/pallas_call | solution.py:529

commit v3 on v2

--- a/solution.py
+++ b/solution.py
@@ -200,7 +200,7 @@
 def gather_kernel(
     left_ref, right_ref, v_ref, m_ref,
     red, vrow, vcol, wrow, wcol,
-    prow, qcol, q_ref, qmid, vmid, lhs, rhs, part_row, part_col, got_row, got_col,
+    prow, qcol, q_ref, qmid, vmid, wmid, lhs, rhs, part, paired, got_pair, got,
     s_p, r_p, s_q, r_q, s_vr, r_vr, s_vc, r_vc, s_wr, r_wr, s_wc, r_wc,
     s_one, r_one, s_two, r_two, s_sum, r_sum,
 ):
@@ -294,7 +294,7 @@
             first_copy(*args, False).start()
 
     for piece in range(PIECES):
-        g_p.start((0, 0), piece)
+        g_p.start((0, 0), piece, ways=("+", "-"))
 
     def relay(gather, own, mid, piece, n):
         rows = pl.ds(piece * gather.depth, gather.depth)
@@ -339,54 +339,47 @@
             rhs[:, pl.ds(256 + n * 128, 128)] = high
             rhs[:, pl.ds(512 + n * 128, 128)] = low
 
-        @pl.loop(0, size // tile)
-        def _(t):
-            rows = pl.ds(pl.multiple_of(t * tile, tile), tile)
-            red[rows, :] += dot(lhs[rows, :], rhs[...], NT)
-
-    row_step(g_vr, (1, 0))
-    row_step(g_vr, (-1, 0))
+        for t in range(size // tile):
+            band = pl.ds(t * tile, tile)
+            red[band, :] += dot(lhs[band, :], rhs[...], NT)
+
+    def rows(*slots, v=True, p=True):
+        for slot in slots:
+            if v:
+                row_step(g_vr, slot)
+            if p:
+                row_step(g_p, slot)
+
+    def cols(*slots):
+        for slot in slots:
+            col_step(g_vc, slot)
+            col_step(g_q, slot)
+
+    rows((1, 0), (-1, 0), p=False)
     for args in crossings:
         relay(*args)
-    for slot in ((0, 1), (1, 0), (-1, 0)):
-        row_step(g_p, slot)
+    for piece in range(PIECES):
+        g_p.start((0, 0), piece, ways=("x",))
+    rows((1, 0), (-1, 0), v=False)
     for args in crossings:
         crossed(*args)
-    for slot in ((2, 0), (-2, 0)):
-        row_step(g_vr, slot)
-        row_step(g_p, slot)
-    row_step(g_vr, (0, 1))
-    for slot in ((0, 0, 1), (1, 0, 0), (-1, 0, 0), (0, 1, 0)):
-        col_step(g_vc, slot)
-        col_step(g_q, slot)
-    for slot in ((3, 0), (-3, 0), (1, 1), (-1, 1)):
-        row_step(g_vr, slot)
-        row_step(g_p, slot)
-    for slot in ((2, 0, 0), (1, 1, 0)):
-        col_step(g_vc, slot)
-        col_step(g_q, slot)
-    for slot in ((2, 1), (-2, 1), (4, 0)):
-        row_step(g_vr, slot)
-        row_step(g_p, slot)
-    for slot in ((-1, 1, 0), (2, 1, 0)):
-        col_step(g_vc, slot)
-        col_step(g_q, slot)
-    for slot in ((1, 0, 1), (-1, 0, 1), (0, 1, 1), (2, 0, 1), (1, 1, 1), (-1, 1, 1), (2, 1, 1)):
-        col_step(g_vc, slot)
-        col_step(g_q, slot)
+    rows((0, 1), (2, 0), (-2, 0))
+    cols((0, 0, 1), (1, 0, 0), (-1, 0, 0), (0, 1, 0))
+    rows(*((3, 0),))
+    cols(*((2, 0, 0),))
+    rows(*((-3, 0),))
+    cols((1, 1, 0), (-1, 1, 0))
+    rows((1, 1), (-1, 1), (2, 1), (-2, 1), (4, 0))
+    cols((2, 1, 0), (1, 0, 1), (-1, 0, 1), (0, 1, 1), (2, 0, 1), (1, 1, 1), (-1, 1, 1), (2, 1, 1))
     accumulate((0, 0), (0, 1))
     accumulate((1, 0), (-1, 0))
     accumulate((2, 0), (-2, 0))
+    accumulate((3, 0), (-3, 0))
     accumulate((1, 1), (-1, 1))
-    accumulate((3, 0), (-3, 0))
     accumulate((2, 1), (-2, 1))
-    for slot in ((3, 1), (-3, 1)):
-        row_step(g_vr, slot)
-        row_step(g_p, slot)
+    rows((3, 1), (-3, 1))
     accumulate((3, 1), (-3, 1))
-    for slot in ((4, 1),):
-        row_step(g_vr, slot)
-        row_step(g_p, slot)
+    rows(*((4, 1),))
     accumulate((4, 0), (4, 1))
 
     high, low = halves(red[...])
@@ -394,58 +387,104 @@
     rhs[...] = low
     width = v_ref.shape[0]
     count = 16 * width
-    vh, vl = halves(vcol[...].reshape(count, size))
-    part_row[...] = (
-        dot(vh, lhs[...], NT) + dot(vh, rhs[...], NT) + dot(vl, lhs[...], NT)
-    ).reshape(16, width, size)
-
-    def addend(buf, got, share, target, n):
+    vh, vl = halves(vrow[...].reshape(count, size))
+    part[...] = -(
+        dot(vh, lhs[...], NN) + dot(vh, rhs[...], NN) + dot(vl, lhs[...], NN)
+    ).reshape(8, 2, width, size)
+
+    pair = pltpu.make_async_remote_copy(
+        src_ref=part.at[:, 1 - at.core],
+        dst_ref=got_pair,
+        send_sem=s_sum.at[7],
+        recv_sem=r_sum.at[7],
+        device_id=at.col_target("c"),
+        device_id_type=MESH,
+    )
+    pair.start()
+    pair.wait_recv()
+    paired[...] = part[:, at.core] + got_pair[...]
+
+    def addend(n):
+        other = lax.rem(i + 2 * n, 16)
         return pltpu.make_async_remote_copy(
-            src_ref=buf.at[share],
-            dst_ref=got.at[n],
-            send_sem=s_sum.at[n + (15 if got is got_col else 0)],
-            recv_sem=r_sum.at[n + (15 if got is got_col else 0)],
-            device_id=target,
+            src_ref=paired.at[at.held(other, c) // 2],
+            dst_ref=got.at[n - 1],
+            send_sem=s_sum.at[n - 1],
+            recv_sem=r_sum.at[n - 1],
+            device_id=(other, c),
             device_id_type=MESH,
         )
 
-    order = (8, 7, 9, 6, 10, 5, 11, 4, 12, 3, 13, 2, 14, 1, 15)
-    for n in order:
-        other = lax.rem(c + n, 16)
-        addend(part_row, got_row, other, (i, other), n - 1).start()
-    vh, vl = halves(vrow[...].reshape(count, size))
-    part_col[...] = -(
-        dot(vh, lhs[...], NN) + dot(vh, rhs[...], NN) + dot(vl, lhs[...], NN)
-    ).reshape(16, width, size)
-    for n in order:
-        other = lax.rem(i + n, 16)
-        addend(part_col, got_col, at.held(other, c), (other, c), n - 1).start()
-
-    def gathered(got, n, sem):
-        pltpu.make_async_copy(got.at[n], got.at[n], r_sum.at[sem]).wait()
-
-    total = part_col[held]
-    for n in range(15):
-        gathered(got_col, n, n + 15)
-        total += got_col[n]
+    for n in (2, 6, 1, 3, 5, 7, 4):
+        addend(n).start()
+    total = paired[opposite]
+    for n in (1, 3, 5, 7, 4, 2, 6):
+        addend(n).wait_recv()
+        total += got[n - 1]
     wcol[held] = total
+
+    last = 1 + PIECES
+    back = pltpu.make_async_remote_copy(
+        src_ref=wcol.at[held],
+        dst_ref=wmid,
+        send_sem=s_two.at[last],
+        recv_sem=r_two.at[last],
+        device_id=beyond,
+        device_id_type=MESH,
+    )
+
+    def home(source_ref):
+        return pltpu.make_async_remote_copy(
+            src_ref=source_ref,
+            dst_ref=wrow.at[at.z * 2 + at.core],
+            send_sem=s_one.at[last],
+            recv_sem=r_one.at[last],
+            device_id=source,
+            device_id_type=MESH,
+        )
+
+    @pl.when(jnp.logical_not(stays))
+    def _():
+        back.start()
+
+    @pl.when(jnp.logical_and(stays, moves))
+    def _():
+        home(wcol.at[held]).start()
+
+    @pl.when(jnp.logical_and(stays, jnp.logical_not(moves)))
+    def _():
+        wrow[c] = wcol[held]
+
     g_wc.start((0, 0, 0), 0)
-    total = part_row[c]
-    for n in range(15):
-        gathered(got_row, n, n)
-        total += got_row[n]
-    wrow[c] = total
+
+    @pl.when(jnp.logical_not(stays))
+    def _():
+        back.wait_recv()
+
+        @pl.when(moves)
+        def _():
+            home(wmid).start()
+
+        @pl.when(jnp.logical_not(moves))
+        def _():
+            wrow[c] = wmid[...]
+
+    for slot in ((1, 0, 0), (-1, 0, 0), (2, 0, 0), (0, 1, 0)):
+        col_step(g_wc, slot)
+
+    @pl.when(moves)
+    def _():
+        pltpu.make_async_copy(wmid, wmid, r_one.at[last]).wait()
+
     g_wr.start((0, 0), 0)
 
-    for slot in ((0, 0, 1), (1, 0, 0), (-1, 0, 0), (2, 0, 0), (0, 1, 0)):
+    for slot in ((1, 1, 0), (-1, 1, 0), (2, 1, 0)):
         col_step(g_wc, slot)
     for slot in ((1, 0), (-1, 0), (2, 0), (-2, 0), (0, 1)):
         row_step(g_wr, slot)
-    for slot in ((1, 1, 0), (-1, 1, 0), (2, 1, 0)):
-        col_step(g_wc, slot)
     for slot in ((3, 0), (-3, 0), (4, 0), (1, 1), (-1, 1), (2, 1), (-2, 1)):
         row_step(g_wr, slot)
-    for slot in COL_SLOTS[9:]:
+    for slot in COL_SLOTS[8:]:
         col_step(g_wc, slot)
     for slot in ((3, 1), (-3, 1), (4, 1)):
         row_step(g_wr, slot)
@@ -465,8 +504,17 @@
             part = mid.at[pl.ds(piece * gather.depth, gather.depth)]
             pltpu.make_async_copy(part, part, s_two.at[n]).wait()
 
-    for n in range(30):
-        pltpu.make_async_copy(got_row.at[0], got_row.at[0], s_sum.at[n]).wait()
+    @pl.when(moves)
+    def _():
+        home(wmid).wait_send()
+
+    @pl.when(jnp.logical_not(stays))
+    def _():
+        back.wait_send()
+
+    for n in range(1, 8):
+        addend(n).wait_send()
+    pair.wait_send()
 
 
 def update_kernel(red, vrow, wrow, vcol, wcol, out, lhs):
@@ -496,7 +544,7 @@
     vmem = pl.BlockSpec(memory_space=pltpu.VMEM)
     dma = pltpu.SemaphoreType.DMA
     small = jax.ShapeDtypeStruct((16, width, size), F32)
-    sems = [dma((16, PIECES))] * 4 + [dma((16, 1))] * 8 + [dma((1 + PIECES,))] * 4 + [dma((30,))] * 2
+    sems = [dma((16, PIECES))] * 4 + [dma((16, 1))] * 8 + [dma((2 + PIECES,))] * 4 + [dma((8,))] * 2
     red, vrow, vcol, wrow, wcol = pl.pallas_call(
         gather_kernel,
         name="gather",
@@ -509,12 +557,13 @@
             pltpu.VMEM((size, 128), F32),
             pltpu.VMEM((size, 128), F32),
             pltpu.VMEM((width, size), F32),
+            pltpu.VMEM((width, size), F32),
             pltpu.VMEM((size, size), BF16),
             pltpu.VMEM((size, size), BF16),
-            pltpu.VMEM((16, width, size), F32),
-            pltpu.VMEM((16, width, size), F32),
-            pltpu.VMEM((15, width, size), F32),
-            pltpu.VMEM((15, width, size), F32),
+            pltpu.VMEM((8, 2, width, size), F32),
+            pltpu.VMEM((8, width, size), F32),
+            pltpu.VMEM((8, width, size), F32),
+            pltpu.VMEM((7, width, size), F32),
         ]
         + sems,
         compiler_params=pltpu.CompilerParams(

time: 148 us -> 131 us (0.89); the launches traced: 145 us -> 130 us
  Pallas kernels: 145 us -> 130 us
    pallas_call x1, Pallas kernels: 139 us -> 124 us  [local(): pl.pallas_call(gather_kernel, name='gather', out_shape=(jax.ShapeDtypeStr...]
where the time goes in v3:
time: 131 us; the launch traced here: 130 us
  Pallas kernels  130 us (99%)
    pallas_call x1, Pallas kernels, local(): pl.pallas_call(gather_kernel, name='gather', out_shape=(jax.ShapeDtypeStr...  124 us
    pallas_call x1, Pallas kernels, local(): pl.pallas_call(update_kernel, name='update', grid=(size // tile,), out_sh...  6.4 us

profile of v3, /device:TPU:8, one launch (start us, length us, event | category | flops | bytes accessed | tf_op | source)
XLA Modules:
  0.0 130.0 jit_solution(16837974795548111285)
XLA Ops:
  0.0 123.6 %gather.1 = (f32[768,768]{1,0:T(8,128)}, f32[16,16,768]{2,1,0:T(8,128)}, f32[16,16,768]{2,1,0:T(8,128)}, f32[16,16,768]{2,1,0:T(8,128)}, f32[16,16,768]{2,1,0:T(8,128)}) custom-call(f32[64,768]{1,0:T(8,128)} %bitcast.11, f32[64,768]{1,0:T(8,128)} %bitcast.12, f32[16,768]{1,0:T(8,128)} %bitcast.13, f32[768,768]{1,0:T(8,128)} %m_ref.1), custom_call_target="tpu_custom_call" | custom-call | tf_op jit(solution)/shard_map/gather/pallas_call | solution.py:548
  123.6 6.4 %update.1 = f32[768,768]{1,0:T(8,128)} custom-call(f32[768,768]{1,0:T(8,128)} %get-tuple-element.10.red, f32[256,768]{1,0:T(8,128)} %bitcast.7, f32[256,768]{1,0:T(8,128)} %bitcast.9, f32[256,768]{1,0:T(8,128)} %bitcast.8, f32[256,768]{1,0:T(8,128)} %bitcast.10), custom_call_target="tpu_custom_call" | custom-call | tf_op jit(solution)/shard_map/update/pallas_call | solution.py:578

commit v4 on v3

--- a/solution.py
+++ b/solution.py
@@ -30,7 +30,7 @@
     (4, 1): (),
 }
 COL_TREE = {
-    (0, 0, 0): (("+", (1, 0, 0)), ("-", (-1, 0, 0)), ("x", (0, 1, 0)), ("c", (0, 0, 1))),
+    (0, 0, 0): (("x", (0, 1, 0)), ("+", (1, 0, 0)), ("-", (-1, 0, 0)), ("c", (0, 0, 1))),
     (1, 0, 0): (("+", (2, 0, 0)), ("c", (1, 0, 1))),
     (-1, 0, 0): (("c", (-1, 0, 1)),),
     (0, 1, 0): (("+", (1, 1, 0)), ("-", (-1, 1, 0)), ("c", (0, 1, 1))),
@@ -139,6 +139,11 @@
         core = lax.rem(i, 2)
         return lax.rem(i // 2 - c // 2 - 4 * core + 16, 8) * 2 + core
 
+    @staticmethod
+    def holder(share, c):
+        core = lax.rem(share, 2)
+        return lax.rem(c // 2 + share // 2 + 4 * core, 8) * 2 + core
+
     def col_target(self, way):
         if way == "x":
             return (((1 - self.lo) * 4 + self.y) * 2 + self.core, self.c)
@@ -199,10 +204,10 @@
 
 def gather_kernel(
     left_ref, right_ref, v_ref, m_ref,
-    red, vrow, vcol, wrow, wcol,
-    prow, qcol, q_ref, qmid, vmid, wmid, lhs, rhs, part, paired, got_pair, got,
+    red,
+    vrow, vcol, wrow, wcol, rhs2, prow, qcol, q_ref, qmid, vmid, wmid, lhs, rhs, part, paired, got_pair, got, tpart, tsum, tpair, tgot, tall, town,
     s_p, r_p, s_q, r_q, s_vr, r_vr, s_vc, r_vc, s_wr, r_wr, s_wc, r_wc,
-    s_one, r_one, s_two, r_two, s_sum, r_sum,
+    s_one, r_one, s_two, r_two, s_sum, r_sum, s_t, r_t, s_all, r_all,
 ):
     at = Place()
     i, c = at.i, at.c
@@ -210,12 +215,6 @@
     tile = 256
 
     barrier = pltpu.get_barrier_semaphore()
-    for n in range(1, 16):
-        other = lax.rem(c + n, 16)
-        pl.semaphore_signal(barrier, inc=1, device_id=(i, other), device_id_type=MESH)
-        other = lax.rem(i + n, 16)
-        pl.semaphore_signal(barrier, inc=1, device_id=(other, c), device_id_type=MESH)
-
     held = at.held(i, c)
     middle = (lax.rem(at.z + i // 2 + 4 * at.hi, 8) * 2 + at.hi, at.z * 2 + at.core)
     opposite = held // 2
@@ -224,10 +223,32 @@
     moves = jnp.logical_or(at.core != at.hi, lax.rem(at.z + 4 * at.hi, 8) != 0)
     stays = opposite == at.z
 
+    def greet(device):
+        pl.semaphore_signal(barrier, inc=1, device_id=device, device_id_type=MESH)
+
+    @pl.when(jnp.logical_not(stays))
+    def _():
+        greet(beyond)
+
     @pl.when(moves)
     def _():
-        pl.semaphore_signal(barrier, inc=1, device_id=middle, device_id_type=MESH)
-        pl.semaphore_signal(barrier, inc=1, device_id=source, device_id_type=MESH)
+        greet(middle)
+        greet(source)
+
+    for way in ("++", "--", "x", "+", "-"):
+        greet(at.row_target(way))
+    for n in range(1, 8):
+        greet((lax.rem(i + 2 * n, 16), c))
+    greet(at.col_target("c"))
+    for n in range(1, 16):
+        j = lax.rem(c + n, 16)
+        greet((at.holder(c, j), j))
+        greet((lax.rem(i + n, 16), held))
+
+    @pl.when(held != c)
+    def _():
+        greet((at.holder(c, c), c))
+        greet((i, held))
 
     left, right = left_ref[...], right_ref[...]
     q_ref[...] = jnp.concatenate([-right, left], axis=0).T
@@ -235,15 +256,13 @@
     vrow[c] = v_ref[...]
     red[...] = m_ref[...]
 
-    @pl.when(moves)
-    def _():
-        pl.semaphore_wait(barrier, 32)
-
     @pl.when(jnp.logical_not(moves))
     def _():
         qmid[...] = q_ref[...]
         vmid[...] = v_ref[...]
-        pl.semaphore_wait(barrier, 30)
+
+    peers = 43 + jnp.where(held != c, 2, 0) + jnp.where(stays, 0, 1) + jnp.where(moves, 2, 0)
+    pl.semaphore_wait(barrier, peers)
 
     @pl.when(jnp.logical_and(jnp.logical_not(moves), stays))
     def _():
@@ -343,66 +362,112 @@
             band = pl.ds(t * tile, tile)
             red[band, :] += dot(lhs[band, :], rhs[...], NT)
 
-    def rows(*slots, v=True, p=True):
+    def run(step, gather, *slots):
         for slot in slots:
-            if v:
-                row_step(g_vr, slot)
-            if p:
-                row_step(g_p, slot)
-
-    def cols(*slots):
-        for slot in slots:
-            col_step(g_vc, slot)
-            col_step(g_q, slot)
-
-    rows((1, 0), (-1, 0), p=False)
-    for args in crossings:
-        relay(*args)
-    for piece in range(PIECES):
-        g_p.start((0, 0), piece, ways=("x",))
-    rows((1, 0), (-1, 0), v=False)
-    for args in crossings:
-        crossed(*args)
-    rows((0, 1), (2, 0), (-2, 0))
-    cols((0, 0, 1), (1, 0, 0), (-1, 0, 0), (0, 1, 0))
-    rows(*((3, 0),))
-    cols(*((2, 0, 0),))
-    rows(*((-3, 0),))
-    cols((1, 1, 0), (-1, 1, 0))
-    rows((1, 1), (-1, 1), (2, 1), (-2, 1), (4, 0))
-    cols((2, 1, 0), (1, 0, 1), (-1, 0, 1), (0, 1, 1), (2, 0, 1), (1, 1, 1), (-1, 1, 1), (2, 1, 1))
-    accumulate((0, 0), (0, 1))
-    accumulate((1, 0), (-1, 0))
-    accumulate((2, 0), (-2, 0))
-    accumulate((3, 0), (-3, 0))
-    accumulate((1, 1), (-1, 1))
-    accumulate((2, 1), (-2, 1))
-    rows((3, 1), (-3, 1))
-    accumulate((3, 1), (-3, 1))
-    rows(*((4, 1),))
-    accumulate((4, 0), (4, 1))
-
-    high, low = halves(red[...])
-    lhs[...] = high
-    rhs[...] = low
+            step(gather, slot)
+
     width = v_ref.shape[0]
     count = 16 * width
-    vh, vl = halves(vrow[...].reshape(count, size))
-    part[...] = -(
-        dot(vh, lhs[...], NN) + dot(vh, rhs[...], NN) + dot(vl, lhs[...], NN)
-    ).reshape(8, 2, width, size)
-
-    pair = pltpu.make_async_remote_copy(
-        src_ref=part.at[:, 1 - at.core],
-        dst_ref=got_pair,
-        send_sem=s_sum.at[7],
-        recv_sem=r_sum.at[7],
-        device_id=at.col_target("c"),
-        device_id_type=MESH,
-    )
-    pair.start()
-    pair.wait_recv()
-    paired[...] = part[:, at.core] + got_pair[...]
+    sibling = at.col_target("c")
+
+    def factor():
+        vh, vl = halves(vrow[...].reshape(count, size))
+        ph, pl_ = halves(prow[c])
+        tpart[...] = (dot(vh, ph, NN) + dot(vh, pl_, NN) + dot(vl, ph, NN)).reshape(8, 2, width, 128)
+        tpaired().start()
+
+    def image_first():
+        vh, vl = halves(vrow[...].reshape(count, size))
+        high, low = halves(m_ref[...])
+        lhs[...] = high
+        rhs[...] = low
+        part[...] = (
+            dot(vh, lhs[...], NN) + dot(vh, rhs[...], NN) + dot(vl, lhs[...], NN)
+        ).reshape(8, 2, width, size)
+
+    def tpaired():
+        return pltpu.make_async_remote_copy(
+            src_ref=tpart.at[:, 1 - at.core],
+            dst_ref=tpair,
+            send_sem=s_t.at[7],
+            recv_sem=r_t.at[7],
+            device_id=sibling,
+            device_id_type=MESH,
+        )
+
+    def taddend(n):
+        other = lax.rem(i + 2 * n, 16)
+        return pltpu.make_async_remote_copy(
+            src_ref=tsum.at[other // 2],
+            dst_ref=tgot.at[n - 1],
+            send_sem=s_t.at[n - 1],
+            recv_sem=r_t.at[n - 1],
+            device_id=(other, c),
+            device_id_type=MESH,
+        )
+
+    def factor_sums():
+        tpaired().wait_recv()
+        tsum[...] = tpart[:, at.core] + tpair[...]
+        for n in (2, 6, 1, 3, 5, 7, 4):
+            taddend(n).start()
+
+    def tspread(n):
+        j = lax.rem(c + n, 16)
+        return pltpu.make_async_remote_copy(
+            src_ref=town,
+            dst_ref=tall.at[i],
+            send_sem=s_all.at[n],
+            recv_sem=r_all.at[i],
+            device_id=(at.holder(c, j), j),
+            device_id_type=MESH,
+        )
+
+    def factor_spread():
+        total = tsum[i // 2]
+        for n in (1, 3, 5, 7, 4, 2, 6):
+            taddend(n).wait_recv()
+            total += tgot[n - 1]
+        town[...] = total
+
+        @pl.when(held != c)
+        def _():
+            tspread(0).start()
+
+        @pl.when(held == c)
+        def _():
+            tall[i] = town[...]
+
+        for n in (8, 7, 9, 6, 10, 5, 11, 4, 12, 3, 13, 2, 14, 1, 15):
+            tspread(n).start()
+
+    def from_row(n):
+        row = lax.rem(i + n, 16)
+        pltpu.make_async_copy(tall.at[row], tall.at[row], r_all.at[row]).wait()
+
+    def image():
+        for n in range(1, 16):
+            from_row(n)
+
+        @pl.when(held != c)
+        def _():
+            from_row(0)
+
+        th, tl = halves(tall[...].reshape(count, 128))
+        qh, ql = halves(qcol[held])
+        more = dot(th, qh, NT) + dot(th, ql, NT) + dot(tl, qh, NT)
+        part[...] = -(part[...] + more.reshape(8, 2, width, size))
+        paired_copy().start()
+
+    def paired_copy():
+        return pltpu.make_async_remote_copy(
+            src_ref=part.at[:, 1 - at.core],
+            dst_ref=got_pair,
+            send_sem=s_sum.at[7],
+            recv_sem=r_sum.at[7],
+            device_id=sibling,
+            device_id_type=MESH,
+        )
 
     def addend(n):
         other = lax.rem(i + 2 * n, 16)
@@ -415,13 +480,11 @@
             device_id_type=MESH,
         )
 
-    for n in (2, 6, 1, 3, 5, 7, 4):
-        addend(n).start()
-    total = paired[opposite]
-    for n in (1, 3, 5, 7, 4, 2, 6):
-        addend(n).wait_recv()
-        total += got[n - 1]
-    wcol[held] = total
+    def image_sums():
+        paired_copy().wait_recv()
+        paired[...] = part[:, at.core] + got_pair[...]
+        for n in (2, 6, 1, 3, 5, 7, 4):
+            addend(n).start()
 
     last = 1 + PIECES
     back = pltpu.make_async_remote_copy(
@@ -443,51 +506,134 @@
             device_id_type=MESH,
         )
 
-    @pl.when(jnp.logical_not(stays))
-    def _():
-        back.start()
-
-    @pl.when(jnp.logical_and(stays, moves))
-    def _():
-        home(wcol.at[held]).start()
-
-    @pl.when(jnp.logical_and(stays, jnp.logical_not(moves)))
-    def _():
-        wrow[c] = wcol[held]
-
-    g_wc.start((0, 0, 0), 0)
-
-    @pl.when(jnp.logical_not(stays))
-    def _():
-        back.wait_recv()
-
+    def image_share():
+        total = paired[opposite]
+        for n in (1, 3, 5, 7, 4, 2, 6):
+            addend(n).wait_recv()
+            total += got[n - 1]
+        wcol[held] = total
+
+        @pl.when(jnp.logical_not(stays))
+        def _():
+            back.start()
+
+        @pl.when(jnp.logical_and(stays, moves))
+        def _():
+            home(wcol.at[held]).start()
+
+        @pl.when(jnp.logical_and(stays, jnp.logical_not(moves)))
+        def _():
+            wrow[c] = wcol[held]
+
+        g_wc.start((0, 0, 0), 0)
+
+    def image_back():
+        @pl.when(jnp.logical_not(stays))
+        def _():
+            back.wait_recv()
+
+            @pl.when(moves)
+            def _():
+                home(wmid).start()
+
+            @pl.when(jnp.logical_not(moves))
+            def _():
+                wrow[c] = wmid[...]
+
+    def image_home():
         @pl.when(moves)
         def _():
-            home(wmid).start()
-
-        @pl.when(jnp.logical_not(moves))
-        def _():
-            wrow[c] = wmid[...]
-
-    for slot in ((1, 0, 0), (-1, 0, 0), (2, 0, 0), (0, 1, 0)):
-        col_step(g_wc, slot)
-
-    @pl.when(moves)
-    def _():
-        pltpu.make_async_copy(wmid, wmid, r_one.at[last]).wait()
-
-    g_wr.start((0, 0), 0)
-
-    for slot in ((1, 1, 0), (-1, 1, 0), (2, 1, 0)):
-        col_step(g_wc, slot)
-    for slot in ((1, 0), (-1, 0), (2, 0), (-2, 0), (0, 1)):
-        row_step(g_wr, slot)
-    for slot in ((3, 0), (-3, 0), (4, 0), (1, 1), (-1, 1), (2, 1), (-2, 1)):
-        row_step(g_wr, slot)
-    for slot in COL_SLOTS[8:]:
-        col_step(g_wc, slot)
-    for slot in ((3, 1), (-3, 1), (4, 1)):
-        row_step(g_wr, slot)
+            pltpu.make_async_copy(wmid, wmid, r_one.at[last]).wait()
+
+        g_wr.start((0, 0), 0)
+
+    def stage(target, flat):
+        high, low = halves(flat)
+        target[:count] = high
+        target[count : 2 * count] = high
+        target[2 * count :] = low
+
+    def outer(rows_ref, right):
+        high, low = halves(rows_ref[...].reshape(count, size).T)
+        lhs[:, :count] = high
+        lhs[:, count : 2 * count] = low
+        lhs[:, 2 * count :] = high
+        for t in range(size // tile):
+            band = pl.ds(t * tile, tile)
+            red[band, :] += dot(lhs[band, :], right[...], NN)
+
+    def first_outer():
+        stage(rhs, wcol[...].reshape(count, size))
+        outer(vrow, rhs)
+        stage(rhs2, -vcol[...].reshape(count, size))
+
+    def last_outer():
+        outer(wrow, rhs2)
+
+    far = lax.rem(opposite - at.z + 8, 8) == 4
+
+    for args in crossings[:1]:
+        relay(*args)
+    run(row_step, g_vr, (2, 0), (-2, 0), (1, 0), (-1, 0))
+    for args in crossings[1:]:
+        relay(*args)
+    run(row_step, g_vr, (3, 0), (-3, 0), (4, 0))
+    run(row_step, g_p, (1, 0), (-1, 0))
+    for piece in range(PIECES):
+        g_p.start((0, 0), piece, ways=("x",))
+
+    @pl.when(jnp.logical_not(far))
+    def _():
+        for args in crossings:
+            crossed(*args)
+
+    run(row_step, g_vr, (0, 1), (1, 1), (-1, 1), (2, 1), (-2, 1), (3, 1), (-3, 1), (4, 1))
+    factor()
+    factor_sums()
+
+    @pl.when(far)
+    def _():
+        for args in crossings:
+            crossed(*args)
+
+    image_first()
+    run(col_step, g_q, (1, 0, 0), (-1, 0, 0), (0, 1, 0))
+    run(row_step, g_p, (0, 1))
+    factor_spread()
+    run(row_step, g_p, (2, 0), (-2, 0))
+    run(col_step, g_vc, (1, 0, 0), (-1, 0, 0), (2, 0, 0))
+    run(col_step, g_q, (1, 1, 0), (-1, 1, 0), (2, 0, 0))
+    image()
+    run(row_step, g_p, (3, 0), (-3, 0))
+    image_sums()
+    run(row_step, g_p, (2, 1), (-2, 1))
+    run(row_step, g_p, (4, 0))
+    run(col_step, g_q, (2, 1, 0))
+    run(col_step, g_vc, (0, 1, 0), (1, 1, 0), (-1, 1, 0), (2, 1, 0))
+    run(col_step, g_q, *COL_SLOTS[8:])
+    run(row_step, g_p, (1, 1), (-1, 1))
+    accumulate((0, 0), (0, 1))
+    image_share()
+    accumulate((1, 0), (-1, 0))
+    accumulate((2, 0), (-2, 0))
+    accumulate((3, 0), (-3, 0))
+    image_back()
+    accumulate((1, 1), (-1, 1))
+    accumulate((2, 1), (-2, 1))
+    run(col_step, g_wc, (1, 0, 0), (-1, 0, 0), (2, 0, 0), (0, 1, 0))
+    image_home()
+    run(row_step, g_p, (3, 1), (-3, 1))
+    run(row_step, g_wr, (1, 0), (-1, 0), (2, 0), (-2, 0))
+    accumulate((3, 1), (-3, 1))
+    run(col_step, g_wc, (1, 1, 0), (-1, 1, 0), (2, 1, 0))
+    run(row_step, g_p, (4, 1))
+    run(row_step, g_wr, (3, 0), (-3, 0), (4, 0))
+    accumulate((4, 0), (4, 1))
+    run(col_step, g_vc, *COL_SLOTS[8:])
+    run(col_step, g_wc, *COL_SLOTS[8:])
+    first_outer()
+    run(row_step, g_wr, (0, 1), (1, 1), (-1, 1), (2, 1), (-2, 1), (3, 1), (-3, 1), (4, 1))
+    last_outer()
 
     for gather in (g_p, g_q, g_vr, g_vc, g_wr, g_wc):
         gather.drain()
@@ -512,46 +658,34 @@
     def _():
         back.wait_send()
 
+    @pl.when(held != c)
+    def _():
+        tspread(0).wait_send()
+
+    for n in range(1, 16):
+        tspread(n).wait_send()
     for n in range(1, 8):
         addend(n).wait_send()
-    pair.wait_send()
-
-
-def update_kernel(red, vrow, wrow, vcol, wcol, out, lhs):
-    count, size = vrow.shape
-
-    @pl.when(pl.program_id(0) == 0)
-    def _():
-        for n, ref in enumerate((vrow, wrow)):
-            high, low = halves(ref[...].T)
-            lhs[:, pl.ds(n * count, count)] = high
-            lhs[:, pl.ds((2 + n) * count, count)] = low
-
-    wh, wl = halves(wcol[...])
-    vh, vl = halves(-vcol[...])
-    high = jnp.concatenate([wh, vh], axis=0)
-    low = jnp.concatenate([wl, vl], axis=0)
-    first = lhs[:, : 2 * count]
-    out[...] = red[...] + (
-        dot(first, high, NN) + dot(first, low, NN) + dot(lhs[:, 2 * count :], high, NN)
-    )
+        taddend(n).wait_send()
+    paired_copy().wait_send()
+    tpaired().wait_send()
 
 
 def local(matrix, left_panel, right_panel, reflectors):
     size = matrix.shape[0]
     width = reflectors.shape[1]
-    count = 16 * width
     vmem = pl.BlockSpec(memory_space=pltpu.VMEM)
     dma = pltpu.SemaphoreType.DMA
-    small = jax.ShapeDtypeStruct((16, width, size), F32)
-    sems = [dma((16, PIECES))] * 4 + [dma((16, 1))] * 8 + [dma((2 + PIECES,))] * 4 + [dma((8,))] * 2
-    red, vrow, vcol, wrow, wcol = pl.pallas_call(
+    sems = [dma((16, PIECES))] * 4 + [dma((16, 1))] * 8 + [dma((2 + PIECES,))] * 4 + [dma((8,))] * 4 + [dma((16,))] * 2
+    return pl.pallas_call(
         gather_kernel,
         name="gather",
-        out_shape=(jax.ShapeDtypeStruct((size, size), F32), small, small, small, small),
+        out_shape=jax.ShapeDtypeStruct((size, size), F32),
         in_specs=[vmem] * 4,
-        out_specs=(vmem,) * 5,
-        scratch_shapes=[
+        out_specs=vmem,
+        scratch_shapes=[pltpu.VMEM((16, width, size), F32)] * 4
+        + [
+            pltpu.VMEM((size, size), BF16),
             pltpu.VMEM((16, size, 128), F32),
             pltpu.VMEM((16, size, 128), F32),
             pltpu.VMEM((size, 128), F32),
@@ -564,27 +698,18 @@
             pltpu.VMEM((8, width, size), F32),
             pltpu.VMEM((8, width, size), F32),
             pltpu.VMEM((7, width, size), F32),
+            pltpu.VMEM((8, 2, width, 128), F32),
+            pltpu.VMEM((8, width, 128), F32),
+            pltpu.VMEM((8, width, 128), F32),
+            pltpu.VMEM((7, width, 128), F32),
+            pltpu.VMEM((16, width, 128), F32),
+            pltpu.VMEM((width, 128), F32),
         ]
         + sems,
         compiler_params=pltpu.CompilerParams(
             collective_id=0, has_side_effects=True, vmem_limit_bytes=56 * 1024 * 1024
         ),
     )(left_panel.T, right_panel.T, reflectors.T, matrix)
-    vrow, vcol, wrow, wcol = (x.reshape(count, size) for x in (vrow, vcol, wrow, wcol))
-    tile = 256
-    whole = pl.BlockSpec((count, size), lambda n: (0, 0))
-    strip = pl.BlockSpec((count, tile), lambda n: (0, n))
-    block = pl.BlockSpec((size, tile), lambda n: (0, n))
-    return pl.pallas_call(
-        update_kernel,
-        name="update",
-        grid=(size // tile,),
-        out_shape=jax.ShapeDtypeStruct((size, size), F32),
-        in_specs=[block, whole, whole, strip, strip],
-        out_specs=block,
-        scratch_shapes=[pltpu.VMEM((size, 4 * count), BF16)],
-        compiler_params=pltpu.CompilerParams(dimension_semantics=("arbitrary",)),
-    )(red, vrow, wrow, vcol, wcol)
 
 
 def solution(mesh):

time: 131 us -> 118 us (0.901)
  Pallas kernels: 130 us -> 115 us
  local copies, waits for them, and re-layouts: 0 us -> 3.22 us
    pallas_call x2 -> x1, Pallas kernels: 130 us -> 115 us  [local(): pl.pallas_call(gather_kernel, name='gather', out_shape=jax.ShapeDtypeStru...]
    unnamed x0 -> x1, local copies, waits for them, and re-layouts: none -> 3.22 us
where the time goes in v4:
time: 118 us
  Pallas kernels  115 us (97%)
  local copies, waits for them, and re-layouts  3.22 us (3%)
    pallas_call x1, Pallas kernels, local(): pl.pallas_call(gather_kernel, name='gather', out_shape=jax.ShapeDtypeStru...  115 us
    unnamed x1, local copies, waits for them, and re-layouts  3.22 us

profile of v4, /device:TPU:8, one launch (start us, length us, event | category | flops | bytes accessed | tf_op | source)
XLA Modules:
  0.0 118.1 jit_solution(5360871189973598725)
XLA Ops:
  0.0 114.9 %gather.1 = f32[768,768]{1,0:T(8,128)} custom-call(f32[64,768]{1,0:T(8,128)} %bitcast.3, f32[64,768]{1,0:T(8,128)} %bitcast.4, f32[16,768]{1,0:T(8,128)} %bitcast.5, f32[768,768]{1,0:T(8,128)} %m_ref.1), custom_call_target="tpu_custom_call" | custom-call | tf_op jit(solution)/shard_map/gather/pallas_call | solution.py:680
  114.9 3.2 %copy.6 = f32[768,768]{1,0:T(8,128)} copy(f32[768,768]{1,0:T(8,128)} %gather.1) | data formatting | bytes 4718592

commit v5 on v4

--- a/solution.py
+++ b/solution.py
@@ -205,7 +205,7 @@
 def gather_kernel(
     left_ref, right_ref, v_ref, m_ref,
     red,
-    vrow, vcol, wrow, wcol, rhs2, prow, qcol, q_ref, qmid, vmid, wmid, lhs, rhs, part, paired, got_pair, got, tpart, tsum, tpair, tgot, tall, town,
+    vrow, vcol, wrow, wcol, rhs2, prow, qcol, q_ref, qmid, vmid, lhs, rhs, part, paired, got_pair, got, tpart, tsum, tpair, tgot, tall, town,
     s_p, r_p, s_q, r_q, s_vr, r_vr, s_vc, r_vc, s_wr, r_wr, s_wc, r_wc,
     s_one, r_one, s_two, r_two, s_sum, r_sum, s_t, r_t, s_all, r_all,
 ):
@@ -222,6 +222,7 @@
     beyond = (i, opposite * 2 + at.hi)
     moves = jnp.logical_or(at.core != at.hi, lax.rem(at.z + 4 * at.hi, 8) != 0)
     stays = opposite == at.z
+    owner = jnp.logical_and(i == c, held == c)
 
     def greet(device):
         pl.semaphore_signal(barrier, inc=1, device_id=device, device_id_type=MESH)
@@ -234,6 +235,11 @@
     def _():
         greet(middle)
         greet(source)
+
+    @pl.when(jnp.logical_not(owner))
+    def _():
+        greet((c, held))
+        greet((at.holder(c, i), i))
 
     for way in ("++", "--", "x", "+", "-"):
         greet(at.row_target(way))
@@ -261,7 +267,7 @@
         qmid[...] = q_ref[...]
         vmid[...] = v_ref[...]
 
-    peers = 43 + jnp.where(held != c, 2, 0) + jnp.where(stays, 0, 1) + jnp.where(moves, 2, 0)
+    peers = 43 + jnp.where(held != c, 2, 0) + jnp.where(stays, 0, 1) + jnp.where(moves, 2, 0) + jnp.where(owner, 0, 2)
     pl.semaphore_wait(barrier, peers)
 
     @pl.when(jnp.logical_and(jnp.logical_not(moves), stays))
@@ -487,22 +493,14 @@
             addend(n).start()
 
     last = 1 + PIECES
-    back = pltpu.make_async_remote_copy(
-        src_ref=wcol.at[held],
-        dst_ref=wmid,
-        send_sem=s_two.at[last],
-        recv_sem=r_two.at[last],
-        device_id=beyond,
-        device_id_type=MESH,
-    )
-
-    def home(source_ref):
-        return pltpu.make_async_remote_copy(
-            src_ref=source_ref,
-            dst_ref=wrow.at[at.z * 2 + at.core],
+
+    def home():
+        return pltpu.make_async_remote_copy(
+            src_ref=wcol.at[held],
+            dst_ref=wrow.at[held],
             send_sem=s_one.at[last],
             recv_sem=r_one.at[last],
-            device_id=source,
+            device_id=(c, held),
             device_id_type=MESH,
         )
 
@@ -513,37 +511,20 @@
             total += got[n - 1]
         wcol[held] = total
 
-        @pl.when(jnp.logical_not(stays))
-        def _():
-            back.start()
-
-        @pl.when(jnp.logical_and(stays, moves))
-        def _():
-            home(wcol.at[held]).start()
-
-        @pl.when(jnp.logical_and(stays, jnp.logical_not(moves)))
+        @pl.when(jnp.logical_not(owner))
+        def _():
+            home().start()
+
+        @pl.when(owner)
         def _():
             wrow[c] = wcol[held]
 
         g_wc.start((0, 0, 0), 0)
 
-    def image_back():
-        @pl.when(jnp.logical_not(stays))
-        def _():
-            back.wait_recv()
-
-            @pl.when(moves)
-            def _():
-                home(wmid).start()
-
-            @pl.when(jnp.logical_not(moves))
-            def _():
-                wrow[c] = wmid[...]
-
     def image_home():
-        @pl.when(moves)
-        def _():
-            pltpu.make_async_copy(wmid, wmid, r_one.at[last]).wait()
+        @pl.when(jnp.logical_not(owner))
+        def _():
+            home().wait_recv()
 
         g_wr.start((0, 0), 0)
 
@@ -570,64 +551,78 @@
     def last_outer():
         outer(wrow, rhs2)
 
-    far = lax.rem(opposite - at.z + 8, 8) == 4
-
     for args in crossings[:1]:
         relay(*args)
     run(row_step, g_vr, (2, 0), (-2, 0), (1, 0), (-1, 0))
     for args in crossings[1:]:
         relay(*args)
+    run(row_step, g_p, (1, 0), (-1, 0))
     run(row_step, g_vr, (3, 0), (-3, 0), (4, 0))
-    run(row_step, g_p, (1, 0), (-1, 0))
     for piece in range(PIECES):
         g_p.start((0, 0), piece, ways=("x",))
-
-    @pl.when(jnp.logical_not(far))
-    def _():
-        for args in crossings:
-            crossed(*args)
-
     run(row_step, g_vr, (0, 1), (1, 1), (-1, 1), (2, 1), (-2, 1), (3, 1), (-3, 1), (4, 1))
     factor()
     factor_sums()
-
-    @pl.when(far)
-    def _():
-        for args in crossings:
-            crossed(*args)
-
+    for args in crossings:
+        crossed(*args)
+    factor_spread()
+    run(row_step, g_p, (2, 0), (-2, 0))
+    run(row_step, g_p, (0, 1))
     image_first()
     run(col_step, g_q, (1, 0, 0), (-1, 0, 0), (0, 1, 0))
-    run(row_step, g_p, (0, 1))
-    factor_spread()
-    run(row_step, g_p, (2, 0), (-2, 0))
-    run(col_step, g_vc, (1, 0, 0), (-1, 0, 0), (2, 0, 0))
-    run(col_step, g_q, (1, 1, 0), (-1, 1, 0), (2, 0, 0))
     image()
+    image_sums()
     run(row_step, g_p, (3, 0), (-3, 0))
-    image_sums()
-    run(row_step, g_p, (2, 1), (-2, 1))
+    run(col_step, g_vc, (1, 0, 0), (-1, 0, 0), (2, 0, 0), (0, 1, 0))
+    run(col_step, g_q, (1, 1, 0), (-1, 1, 0), (2, 0, 0), *COL_SLOTS[8:15])
+    run(row_step, g_p, (1, 1), (-1, 1))
+
+    late = (at.col_share((2, 1, 0)), at.col_share((2, 1, 1)))
+    pairs = (((0, 0), (0, 1)), ((1, 0), (-1, 0)), ((2, 0), (-2, 0)), ((3, 0), (-3, 0)), ((1, 1), (-1, 1)))
+
+    def ready(n):
+        is_ready = None
+        for slot in pairs[n]:
+            for share in late:
+                test = at.row_share(slot) != share
+                is_ready = test if is_ready is None else jnp.logical_and(is_ready, test)
+        return is_ready
+
+    def early(*numbers):
+        for n in numbers:
+
+            @pl.when(ready(n))
+            def _():
+                accumulate(*pairs[n])
+
+    def remaining():
+        for n in range(len(pairs)):
+
+            @pl.when(jnp.logical_not(ready(n)))
+            def _():
+                accumulate(*pairs[n])
+
+    early(0)
+    run(row_step, g_p, (2, 1))
+    early(1)
+    run(row_step, g_p, (-2, 1))
+    early(2)
     run(row_step, g_p, (4, 0))
-    run(col_step, g_q, (2, 1, 0))
-    run(col_step, g_vc, (0, 1, 0), (1, 1, 0), (-1, 1, 0), (2, 1, 0))
-    run(col_step, g_q, *COL_SLOTS[8:])
-    run(row_step, g_p, (1, 1), (-1, 1))
-    accumulate((0, 0), (0, 1))
+    early(3)
     image_share()
-    accumulate((1, 0), (-1, 0))
-    accumulate((2, 0), (-2, 0))
-    accumulate((3, 0), (-3, 0))
-    image_back()
-    accumulate((1, 1), (-1, 1))
+    early(4)
+    run(col_step, g_q, (2, 1, 0), (2, 1, 1))
+    remaining()
+    run(col_step, g_wc, (1, 0, 0), (-1, 0, 0), (2, 0, 0))
+    image_home()
     accumulate((2, 1), (-2, 1))
-    run(col_step, g_wc, (1, 0, 0), (-1, 0, 0), (2, 0, 0), (0, 1, 0))
-    image_home()
+    run(row_step, g_wr, (1, 0), (-1, 0), (2, 0), (-2, 0))
     run(row_step, g_p, (3, 1), (-3, 1))
-    run(row_step, g_wr, (1, 0), (-1, 0), (2, 0), (-2, 0))
     accumulate((3, 1), (-3, 1))
-    run(col_step, g_wc, (1, 1, 0), (-1, 1, 0), (2, 1, 0))
+    run(row_step, g_wr, (3, 0), (-3, 0), (4, 0))
     run(row_step, g_p, (4, 1))
-    run(row_step, g_wr, (3, 0), (-3, 0), (4, 0))
+    run(col_step, g_vc, (1, 1, 0), (-1, 1, 0), (2, 1, 0))
+    run(col_step, g_wc, (0, 1, 0), (1, 1, 0), (-1, 1, 0), (2, 1, 0))
     accumulate((4, 0), (4, 1))
     run(col_step, g_vc, *COL_SLOTS[8:])
     run(col_step, g_wc, *COL_SLOTS[8:])
@@ -650,13 +645,9 @@
             part = mid.at[pl.ds(piece * gather.depth, gather.depth)]
             pltpu.make_async_copy(part, part, s_two.at[n]).wait()
 
-    @pl.when(moves)
-    def _():
-        home(wmid).wait_send()
-
-    @pl.when(jnp.logical_not(stays))
-    def _():
-        back.wait_send()
+    @pl.when(jnp.logical_not(owner))
+    def _():
+        home().wait_send()
 
     @pl.when(held != c)
     def _():
@@ -671,13 +662,18 @@
     tpaired().wait_send()
 
 
+def copy_kernel(source, out):
+    out[...] = source[...]
+
+
 def local(matrix, left_panel, right_panel, reflectors):
     size = matrix.shape[0]
     width = reflectors.shape[1]
     vmem = pl.BlockSpec(memory_space=pltpu.VMEM)
     dma = pltpu.SemaphoreType.DMA
     sems = [dma((16, PIECES))] * 4 + [dma((16, 1))] * 8 + [dma((2 + PIECES,))] * 4 + [dma((8,))] * 4 + [dma((16,))] * 2
-    return pl.pallas_call(
+    block = pl.BlockSpec((size // 4, size), lambda n: (n, 0))
+    updated = pl.pallas_call(
         gather_kernel,
         name="gather",
         out_shape=jax.ShapeDtypeStruct((size, size), F32),
@@ -690,7 +686,6 @@
             pltpu.VMEM((16, size, 128), F32),
             pltpu.VMEM((size, 128), F32),
             pltpu.VMEM((size, 128), F32),
-            pltpu.VMEM((width, size), F32),
             pltpu.VMEM((width, size), F32),
             pltpu.VMEM((size, size), BF16),
             pltpu.VMEM((size, size), BF16),
@@ -710,6 +705,14 @@
             collective_id=0, has_side_effects=True, vmem_limit_bytes=56 * 1024 * 1024
         ),
     )(left_panel.T, right_panel.T, reflectors.T, matrix)
+    return pl.pallas_call(
+        copy_kernel,
+        name="hand_over",
+        grid=(4,),
+        out_shape=jax.ShapeDtypeStruct((size, size), F32),
+        in_specs=[block],
+        out_specs=block,
+    )(updated)
 
 
 def solution(mesh):

time: 118 us -> 112 us (0.949); the launches traced: 118 us -> 111 us
  Pallas kernels: 115 us -> 111 us
  local copies, waits for them, and re-layouts: 3.22 us -> 0 us
    pallas_call x1, Pallas kernels: 115 us -> 107 us  [local(): pl.pallas_call(gather_kernel, name='gather', out_shape=jax.ShapeDtypeStru...]
    pallas_call x0 -> x1, Pallas kernels: none -> 3.88 us  [local(): pl.pallas_call(copy_kernel, name='hand_over', grid=(4,), out_shape=jax.Sh...]
    unnamed x1 -> x0, local copies, waits for them, and re-layouts: 3.22 us -> none
where the time goes in v5:
time: 112 us; the launch traced here: 111 us
  Pallas kernels  111 us (99%)
    pallas_call x1, Pallas kernels, local(): pl.pallas_call(gather_kernel, name='gather', out_shape=jax.ShapeDtypeStru...  107 us
    pallas_call x1, Pallas kernels, local(): pl.pallas_call(copy_kernel, name='hand_over', grid=(4,), out_shape=jax.Sh...  3.88 us

profile of v5, /device:TPU:8, one launch (start us, length us, event | category | flops | bytes accessed | tf_op | source)
XLA Modules:
  0.0 110.8 jit_solution(15984953399556777524)
XLA Ops:
  0.0 106.9 %gather.1.source = f32[768,768]{1,0:T(8,128)} custom-call(f32[64,768]{1,0:T(8,128)} %bitcast.3, f32[64,768]{1,0:T(8,128)} %bitcast.4, f32[16,768]{1,0:T(8,128)} %bitcast.5, f32[768,768]{1,0:T(8,128)} %m_ref.1), custom_call_target="tpu_custom_call" | custom-call | tf_op jit(solution)/shard_map/gather/pallas_call | solution.py:676
  106.9 3.9 %hand_over.1 = f32[768,768]{1,0:T(8,128)} custom-call(f32[768,768]{1,0:T(8,128)} %gather.1.source), custom_call_target="tpu_custom_call" | custom-call | tf_op jit(solution)/shard_map/hand_over/pallas_call | solution.py:708

commit v6 on v5

--- a/solution.py
+++ b/solution.py
@@ -662,18 +662,13 @@
     tpaired().wait_send()
 
 
-def copy_kernel(source, out):
-    out[...] = source[...]
-
-
 def local(matrix, left_panel, right_panel, reflectors):
     size = matrix.shape[0]
     width = reflectors.shape[1]
     vmem = pl.BlockSpec(memory_space=pltpu.VMEM)
     dma = pltpu.SemaphoreType.DMA
     sems = [dma((16, PIECES))] * 4 + [dma((16, 1))] * 8 + [dma((2 + PIECES,))] * 4 + [dma((8,))] * 4 + [dma((16,))] * 2
-    block = pl.BlockSpec((size // 4, size), lambda n: (n, 0))
-    updated = pl.pallas_call(
+    return pl.pallas_call(
         gather_kernel,
         name="gather",
         out_shape=jax.ShapeDtypeStruct((size, size), F32),
@@ -705,14 +700,6 @@
             collective_id=0, has_side_effects=True, vmem_limit_bytes=56 * 1024 * 1024
         ),
     )(left_panel.T, right_panel.T, reflectors.T, matrix)
-    return pl.pallas_call(
-        copy_kernel,
-        name="hand_over",
-        grid=(4,),
-        out_shape=jax.ShapeDtypeStruct((size, size), F32),
-        in_specs=[block],
-        out_specs=block,
-    )(updated)
 
 
 def solution(mesh):

time: 112 us -> 111 us (level)
  Pallas kernels: 111 us -> 107 us
  local copies, waits for them, and re-layouts: 0 us -> 3.22 us
    pallas_call x1 -> x0, Pallas kernels: 3.88 us -> none  [local(): pl.pallas_call(copy_kernel, name='hand_over', grid=(4,), out_shape=jax.Sh...]
    unnamed x0 -> x1, local copies, waits for them, and re-layouts: none -> 3.22 us
where the time goes in v6:
time: 111 us; the launch traced here: 110 us
  Pallas kernels  107 us (96%)
  local copies, waits for them, and re-layouts  3.22 us (3%)
    pallas_call x1, Pallas kernels, local(): pl.pallas_call(gather_kernel, name='gather', out_shape=jax.ShapeDtypeStru...  107 us
    unnamed x1, local copies, waits for them, and re-layouts  3.22 us

profile of v6, /device:TPU:8, one launch (start us, length us, event | category | flops | bytes accessed | tf_op | source)
XLA Modules:
  0.0 110.2 jit_solution(13021907845564540926)
XLA Ops:
  0.0 106.9 %gather.1 = f32[768,768]{1,0:T(8,128)} custom-call(f32[64,768]{1,0:T(8,128)} %bitcast.3, f32[64,768]{1,0:T(8,128)} %bitcast.4, f32[16,768]{1,0:T(8,128)} %bitcast.5, f32[768,768]{1,0:T(8,128)} %m_ref.1), custom_call_target="tpu_custom_call" | custom-call | tf_op jit(solution)/shard_map/gather/pallas_call | solution.py:671
  106.9 3.2 %copy.6 = f32[768,768]{1,0:T(8,128)} copy(f32[768,768]{1,0:T(8,128)} %gather.1) | data formatting | bytes 4718592
